TPU v7x, 32 devices: a 4x4x1 block of a 4x4x8 slice. The times are simulated.
32 devices in a mesh: data: 1 (over z), pp: 4 (over y), ep: 8 (over x, core).
Axes of the slice: x: 4, y: 4, z: 1, core: 2. Of those that a mesh axis runs over, the one named last changes fastest.
The devices are a block of a 4x4x8 slice.
Arguments:
- expert_out: bfloat16 [4, 2, 256, 128, 2048], P('pp', 'data', 'ep')
- expert_ids: int32 [4, 2, 32, 64, 8], P('pp', 'data', 'ep')
- slot_ids: int32 [4, 2, 32, 64, 8], P('pp', 'data', 'ep')
- gate_weights: float32 [4, 2, 32, 64, 8], P('pp', 'data', 'ep')
- residual: bfloat16 [4, 2, 32, 64, 2048], P('pp', 'data', 'ep')
- norm_moe: float32 [4, 2048], P('pp')
- w_gate: bfloat16 [4, 2048, 512], P('pp')
- w_up: bfloat16 [4, 2048, 512], P('pp')
- w_down: bfloat16 [4, 512, 2048], P('pp')
- norm_attn: float32 [4, 2048], P('pp')
- w_query: bfloat16 [4, 2048, 16, 128], P('pp')
- w_key: bfloat16 [4, 2048, 16, 128], P('pp')
- w_value: bfloat16 [4, 2048, 16, 128], P('pp')
- w_out: bfloat16 [4, 16, 128, 2048], P('pp')
Outputs:
- output: bfloat16 [4, 2, 32, 64, 2048], P('pp', 'data', 'ep')
All inputs are finite; a program needn't handle non-finite values.
Results may differ from a plain program's by a relative error of at most 0.0154484.
Values are sent between devices in bfloat16 or wider.
A program may use at most 768 MiB of HBM per device.

v0:
```python
import math
import jax
import jax.numpy as jnp
from jax import lax
from jax.sharding import PartitionSpec as P

EPSILON = 1e-6


def rms_norm(tensor, gain):
    values = tensor.astype(jnp.float32)
    inv_rms = lax.rsqrt(jnp.mean(values * values, axis=-1, keepdims=True) + EPSILON)
    return values * inv_rms * gain


def shared_expert(residual, norm_moe, w_gate, w_up, w_down):
    normed = rms_norm(residual, norm_moe).astype(jnp.bfloat16)
    gate_act = jnp.einsum("bld,df->blf", normed, w_gate, preferred_element_type=jnp.float32)
    up_act = jnp.einsum("bld,df->blf", normed, w_up, preferred_element_type=jnp.float32)
    hidden = (jax.nn.silu(gate_act) * up_act).astype(jnp.bfloat16)
    return jnp.einsum("blf,fd->bld", hidden, w_down, preferred_element_type=jnp.float32).astype(jnp.bfloat16)


def gather_combine(row_table, row_ids, kept_mask, gate_weights):
    picked = jnp.take(row_table, row_ids, axis=0, mode="clip")
    weights = jnp.where(kept_mask, gate_weights, 0.0)
    return jnp.sum(picked.astype(jnp.float32) * weights[..., None], axis=-2)


def attention_block(combined, norm_attn, w_query, w_key, w_value, w_out):
    seq_len = combined.shape[1]
    score_scale = 1.0 / math.sqrt(w_query.shape[2])
    normed = rms_norm(combined, norm_attn).astype(jnp.bfloat16)
    queries = jnp.einsum("bld,dhe->blhe", normed, w_query, preferred_element_type=jnp.float32).astype(jnp.bfloat16)
    key_heads = jnp.einsum("bld,dhe->blhe", normed, w_key, preferred_element_type=jnp.float32).astype(jnp.bfloat16)
    value_heads = jnp.einsum("bld,dhe->blhe", normed, w_value, preferred_element_type=jnp.float32).astype(jnp.bfloat16)
    scores = jnp.einsum("bqhe,bkhe->bhqk", queries, key_heads, preferred_element_type=jnp.float32) * score_scale
    causal = jnp.arange(seq_len)[:, None] >= jnp.arange(seq_len)[None, :]
    scores = jnp.where(causal, scores, -1e30)
    attn_probs = jnp.exp(scores - jnp.max(scores, axis=-1, keepdims=True))
    prob_sum = jnp.sum(attn_probs, axis=-1, keepdims=True)
    attn_mixed = jnp.einsum("bhqk,bkhe->bhqe", attn_probs.astype(jnp.bfloat16), value_heads, preferred_element_type=jnp.float32) / prob_sum
    attn_proj = jnp.einsum("cirf,ife->cre", attn_mixed.astype(jnp.bfloat16), w_out, preferred_element_type=jnp.float32).astype(jnp.bfloat16)
    return (combined.astype(jnp.float32) + attn_proj.astype(jnp.float32)).astype(jnp.bfloat16)


def solution(mesh):
    stages = mesh.shape["pp"]
    ep_size = mesh.shape["ep"]
    shift_pairs = [(source, (source + 1) % stages) for source in range(stages)]
    tok_spec = P("pp", "data", "ep", None, None)
    vec_spec = P("pp", None)
    mat_spec = P("pp", None, None)
    head_spec = P("pp", None, None, None)

    def device_step(expert_out, expert_ids, slot_ids, gate_weights, residual, norm_moe, w_gate, w_up, w_down, norm_attn, w_query, w_key, w_value, w_out):
        micro_count = expert_out.shape[1]
        local_experts, slots_total, model_dim = expert_out.shape[2:]
        cap_slots = slots_total // ep_size
        first_slot = lax.axis_index("ep") * cap_slots
        results = []
        for micro_idx in range(micro_count):
            local_out = expert_out[0, micro_idx].reshape(local_experts, ep_size, cap_slots, model_dim)
            received = lax.all_to_all(local_out, "ep", 1, 0, tiled=True)
            row_table = received.reshape(local_experts * ep_size * cap_slots, model_dim)
            slot_here = slot_ids[0, micro_idx]
            kept_mask = slot_here >= 0
            row_ids = expert_ids[0, micro_idx] * cap_slots + jnp.where(kept_mask, slot_here - first_slot, 0)
            routed = gather_combine(row_table, row_ids, kept_mask, gate_weights[0, micro_idx])
            resid_here = residual[0, micro_idx]
            shared = shared_expert(resid_here, norm_moe[0], w_gate[0], w_up[0], w_down[0])
            combined = (resid_here.astype(jnp.float32) + shared.astype(jnp.float32) + routed).astype(jnp.bfloat16)
            incoming = lax.ppermute(combined, "pp", shift_pairs)
            results.append(attention_block(incoming, norm_attn[0], w_query[0], w_key[0], w_value[0], w_out[0]))
        return jnp.stack(results)[None]

    in_specs = (tok_spec,) * 5 + (vec_spec, mat_spec, mat_spec, mat_spec, vec_spec, head_spec, head_spec, head_spec, head_spec)
    return jax.shard_map(device_step, mesh=mesh, in_specs=in_specs, out_specs=tok_spec, check_vma=False)
```

profile of v0, /device:TPU:97, one launch (start us, length us, event | category | flops | bytes accessed | tf_op | source)
XLA Modules:
  0.0 538.1 jit_solution(17777181163361741826)
XLA Ops:
  0.0 0.0 copy-start
  0.0 18.6 %fusion.190 = (bf16[1,1,32,128,2048]{4,3,2,1,0:T(8,128)(2,1)S(1)}, bf16[1,1,32,128,2048]{4,3,2,1,0:T(8,128)(2,1)}) fusion(bf16[1,2,32,128,2048]{4,3,2,1,0:T(8,128)(2,1)} %param.14), kind=kLoop, calls=%fused_computation.148 | loop fusion | bytes 67108864 | tf_op jit(solution)/shard_map/slice | solution.py:63
  18.6 6.9 %copy.19 = bf16[32,8,16,2048]{3,2,0,1:T(8,128)(2,1)} copy(bf16[32,8,16,2048]{3,2,1,0:T(8,128)(2,1)S(1)} %bitcast.183) | data formatting | bytes 33554432 | tf_op jit(solution)/shard_map/reshape;squeeze | solution.py:63
  25.5 7.6 %all-to-all-start = ((bf16[32,8,16,2048]{3,2,0,1:T(8,128)(2,1)}), bf16[32,8,16,2048]{3,2,0,1:T(8,128)(2,1)}, u32[]{:S(2)}, u32[]{:S(2)}) async-start(bf16[32,8,16,2048]{3,2,0,1:T(8,128)(2,1)} %copy.19), calls=%async_computation | async-start | bytes 33554432 | tf_op jit(solution)/shard_map/all_to_all | solution.py:64
  33.1 14.1 %copy.22 = bf16[32,8,16,2048]{3,2,0,1:T(8,128)(2,1)} copy(bf16[32,8,16,2048]{3,2,1,0:T(8,128)(2,1)} %bitcast.182) | data formatting | bytes 33554432 | tf_op jit(solution)/shard_map/reshape;squeeze | solution.py:63
  47.3 169.4 %all-to-all-done = bf16[32,8,16,2048]{3,2,0,1:T(8,128)(2,1)} async-done(((bf16[32,8,16,2048]{3,2,0,1:T(8,128)(2,1)}), bf16[32,8,16,2048]{3,2,0,1:T(8,128)(2,1)}, u32[]{:S(2)}, u32[]{:S(2)}) %all-to-all-start) | async-done | bytes 16777248 | tf_op jit(solution)/shard_map/all_to_all | solution.py:64
  216.6 6.7 %all-to-all-start.1 = ((bf16[32,8,16,2048]{3,2,0,1:T(8,128)(2,1)}), bf16[32,8,16,2048]{3,2,0,1:T(8,128)(2,1)}, u32[]{:S(2)}, u32[]{:S(2)}) async-start(bf16[32,8,16,2048]{3,2,0,1:T(8,128)(2,1)} %copy.22), calls=%async_computation.1 | async-start | bytes 33554432 | tf_op jit(solution)/shard_map/all_to_all | solution.py:64
  223.3 0.0 copy-done.4
  223.3 0.0 copy-done.5
  223.4 0.1 copy.21
  223.5 0.1 copy.20
  223.6 0.1 reshape.172
  223.7 0.1 copy.24
  223.8 0.1 copy.23
  223.9 0.1 reshape.180
  224.0 0.0 copy-start.1
  224.0 2.2 fusion.62
  226.3 0.0 copy-start.7
  226.3 2.5 fusion.82
  228.8 0.0 copy-done.7
  228.8 1.6 fusion.80
  230.3 24.7 %gather_fusion = bf16[2048,2048]{1,0:T(8,128)(2,1)} fusion(bf16[4096,2048]{1,0:T(8,128)(2,1)} %bitcast.12, s32[2048]{0:T(1024)S(1)} %broadcast_clamp_fusion.1), kind=kCustom, calls=%fused_computation | custom fusion | bytes 16785408 | tf_op jit(solution)/shard_map/jit(_take)/gather | solution.py:25
  255.0 12.2 %fusion.1 = f32[4,64,2048]{2,1,0:T(8,128)} fusion(f32[4,64,8]{2,1,0:T(8,128)S(1)} %copy.21, bf16[2048,2048]{1,0:T(8,128)(2,1)} %gather_fusion), kind=kLoop, calls=%fused_computation.5 | loop fusion | flops 12058624 | bytes 10493952 | tf_op jit(solution)/shard_map/reduce_sum | solution.py:27
  267.3 5.2 fusion.30
  272.5 1.3 collective-permute-start
  273.7 133.1 %all-to-all-done.1 = bf16[32,8,16,2048]{3,2,0,1:T(8,128)(2,1)} async-done(((bf16[32,8,16,2048]{3,2,0,1:T(8,128)(2,1)}), bf16[32,8,16,2048]{3,2,0,1:T(8,128)(2,1)}, u32[]{:S(2)}, u32[]{:S(2)}) %all-to-all-start.1) | async-done | bytes 16777248 | tf_op jit(solution)/shard_map/all_to_all | solution.py:64
  406.8 24.4 %gather_fusion.1 = bf16[2048,2048]{1,0:T(8,128)(2,1)} fusion(bf16[4096,2048]{1,0:T(8,128)(2,1)} %bitcast.35, s32[2048]{0:T(1024)S(1)} %broadcast_clamp_fusion), kind=kCustom, calls=%fused_computation.1 | custom fusion | bytes 16785408 | tf_op jit(solution)/shard_map/jit(_take)/gather | solution.py:25
  431.2 12.2 %fusion = f32[4,64,2048]{2,1,0:T(8,128)} fusion(f32[4,64,8]{2,1,0:T(8,128)S(1)} %copy.24, bf16[2048,2048]{1,0:T(8,128)(2,1)} %gather_fusion.1), kind=kLoop, calls=%fused_computation.3 | loop fusion | flops 12058624 | bytes 10493952 | tf_op jit(solution)/shard_map/reduce_sum | solution.py:27
  443.5 5.4 %fusion.33 = bf16[4,64,2048]{2,1,0:T(8,128)(2,1)} fusion(f32[4,64,2048]{2,1,0:T(8,128)} %fusion, bf16[1,512,2048]{2,1,0:T(8,128)(2,1)S(1)} %copy-done, bf16[1,2,4,64,2048]{4,3,2,1,0:T(8,128)(2,1)} %param.18, bf16[1,2048,512]{2,1,0:T(8,128)(2,1)} %param.21, f32[4,64]{1,0:T(4,128)S(1)} %add_rsqrt_fusion.1, f32[2048]{0:T(1024)S(1)} %bitcast.195, ...), kind=kOutput, calls=%fused_computation.45 | convolution fusion | flops 1079771136 | bytes 9970688 | tf_op jit(solution)/shard_map/blf,fd->bld/dot_general | solution.py:21
  448.9 1.4 collective-permute-start.1
  450.3 0.0 collective-permute-done
  450.3 0.3 fusion.68
  450.6 24.7 %collective-permute-done.1 = bf16[4,64,2048]{2,1,0:T(8,128)(2,1)S(1)} collective-permute-done((bf16[4,64,2048]{2,1,0:T(8,128)(2,1)}, bf16[4,64,2048]{2,1,0:T(8,128)(2,1)S(1)}, u32[]{:S(2)}, u32[]{:S(2)}) %collective-permute-start.1) | collective-permute-done | bytes 1048608 | tf_op jit(solution)/shard_map/ppermute | solution.py:73
  475.3 0.3 fusion.71
  475.6 0.0 copy-done.9
  475.6 6.0 %fusion.8 = bf16[4,64,16,128]{3,1,2,0:T(8,128)(2,1)S(1)} fusion(bf16[2048,16,128,1]{2,1,0,3:T(8,128)(2,1)} %bitcast.184, bf16[4,64,2048]{2,1,0:T(8,128)(2,1)S(1)} %collective-permute-done, f32[2048]{0:T(1024)S(1)} %bitcast.196, f32[4,64]{1,0:T(4,128)S(1)} %add_rsqrt_fusion.2), kind=kOutput, calls=%fused_computation.12 | convolution fusion | flops 2149580800 | bytes 10494976 | tf_op jit(solution)/shard_map/bld,dhe->blhe/dot_general | solution.py:36
  481.6 1.7 copy.69
  483.3 6.0 %fusion.6 = bf16[4,64,16,128]{3,1,2,0:T(8,128)(2,1)S(1)} fusion(bf16[2048,16,128,1]{2,1,0,3:T(8,128)(2,1)} %bitcast.185, bf16[4,64,2048]{2,1,0:T(8,128)(2,1)S(1)} %collective-permute-done.1, f32[4,64]{1,0:T(4,128)S(1)} %add_rsqrt_fusion, f32[2048]{0:T(1024)S(1)} %bitcast.197), kind=kOutput, calls=%fused_computation.10 | convolution fusion | flops 2149580800 | bytes 10494976 | tf_op jit(solution)/shard_map/bld,dhe->blhe/dot_general | solution.py:36
  489.2 1.7 copy.68
  490.9 0.0 slice-done
  490.9 3.5 fusion.90
  494.4 3.5 fusion.93
  497.9 8.3 %fusion.84 = (f32[4,16,64]{2,1,0:T(8,128)S(1)}, f32[4,16,64,64]{2,3,1,0:T(8,128)}) fusion(pred[64,64]{0,1:T(8,128)(4,1)S(1)} %iota_compare_fusion, bf16[4,64,16,128]{3,1,2,0:T(8,128)(2,1)} %fusion.90, bf16[2048,16,128,1]{2,1,0,3:T(8,128)(2,1)} %bitcast.190, bf16[4,64,2048]{2,1,0:T(8,128)(2,1)S(1)} %collective-permute-done, f32[2048]{0:T(1024)S(1)} %bitcast.200, ...), kind=kOutput, calls=%fused_computation.85 | convolution fusion | flops 2217996288 | bytes 11564032 | tf_op jit(solution)/shard_map/bqhe,bkhe->bhqk/dot_general | solution.py:37
  506.2 9.5 %fusion.86 = (f32[4,16,64]{2,1,0:T(8,128)S(1)}, f32[4,16,64]{2,1,0:T(8,128)S(1)}, f32[4,16,64,64]{2,3,1,0:T(8,128)}) fusion(f32[4,16,64,64]{2,3,1,0:T(8,128)} %get-tuple-element.20, f32[4,16,64]{2,1,0:T(8,128)S(1)} %get-tuple-element.19, pred[64,64]{0,1:T(8,128)(4,1)S(1)} %iota_compare_fusion, bf16[4,64,16,128]{3,1,2,0:T(8,128)(2,1)} %fusion.93, ...), kind=kOutput, calls=%fused_computation.87 | convolution fusion | flops 2219040768 | bytes 12645376 | tf_op jit(solution)/shard_map/bqhe,bkhe->bhqk/dot_general | solution.py:37
  515.6 2.2 fusion.88
  517.8 8.4 %fusion.59 = bf16[1,4,64,2048]{3,2,1,0:T(8,128)(2,1)} fusion(bf16[1,16,128,2048]{3,2,1,0:T(8,128)(2,1)} %param.27, bf16[4,64,2048]{2,1,0:T(8,128)(2,1)S(1)} %collective-permute-done, f32[4,16,64,64]{2,3,1,0:T(8,128)} %get-tuple-element.20, bf16[4,64,16,128]{3,2,1,0:T(8,128)(2,1)} %copy.69, f32[4,16,64]{2,1,0:T(8,128)S(1)} %get-tuple-element.7, ...), kind=kOutput, calls=%fused_computation.53 | convolution fusion | flops 2219311104 | bytes 12619776 | tf_op jit(solution)/shard_map/cirf,ife->cre/dot_general | solution.py:43
  526.2 8.6 %fusion.56 = bf16[1,4,64,2048]{3,2,1,0:T(8,128)(2,1)} fusion(bf16[1,16,128,2048]{3,2,1,0:T(8,128)(2,1)} %param.27, bf16[4,64,2048]{2,1,0:T(8,128)(2,1)} %copy-done.2, f32[4,16,64,64]{2,3,1,0:T(8,128)} %get-tuple-element.21, bf16[4,64,16,128]{3,2,1,0:T(8,128)(2,1)} %copy.68, f32[4,16,64]{2,1,0:T(8,128)S(1)} %fusion.88, ...), kind=kOutput, calls=%fused_computation.52 | convolution fusion | flops 2219311104 | bytes 12619776 | tf_op jit(solution)/shard_map/cirf,ife->cre/dot_general | solution.py:43
  534.9 2.7 maximum_bitcast_fusion
  (26 shorter events, 0.1 us)
Async XLA Ops:
  0.0 267.3 %copy-start = (bf16[1,512,2048]{2,1,0:T(8,128)(2,1)S(1)}, bf16[1,512,2048]{2,1,0:T(8,128)(2,1)}, u32[]{:S(2)}) copy-start(bf16[1,512,2048]{2,1,0:T(8,128)(2,1)} %param.22) | copy-start | bytes 6291460
  25.5 191.1 %all-to-all-start = ((bf16[32,8,16,2048]{3,2,0,1:T(8,128)(2,1)}), bf16[32,8,16,2048]{3,2,0,1:T(8,128)(2,1)}, u32[]{:S(2)}, u32[]{:S(2)}) async-start(bf16[32,8,16,2048]{3,2,0,1:T(8,128)(2,1)} %copy.19), calls=%async_computation | async-start | bytes 33554432 | tf_op jit(solution)/shard_map/all_to_all | solution.py:64
  47.2 176.1 %copy-start.4 = (s32[1,2,4,64,8]{3,4,2,1,0:T(8,128)S(1)}, s32[1,2,4,64,8]{3,4,2,1,0:T(8,128)}, u32[]{:S(2)}) copy-start(s32[1,2,4,64,8]{3,4,2,1,0:T(8,128)} %param.15) | copy-start | bytes 49156
  47.2 176.1 %copy-start.5 = (s32[1,2,4,64,8]{3,4,2,1,0:T(8,128)S(1)}, s32[1,2,4,64,8]{3,4,2,1,0:T(8,128)}, u32[]{:S(2)}) copy-start(s32[1,2,4,64,8]{3,4,2,1,0:T(8,128)} %param.16) | copy-start | bytes 49156
  47.2 176.1 %copy-start.6 = (f32[1,2,4,64,8]{3,4,2,1,0:T(8,128)S(1)}, f32[1,2,4,64,8]{3,4,2,1,0:T(8,128)}, u32[]{:S(2)}) copy-start(f32[1,2,4,64,8]{3,4,2,1,0:T(8,128)} %param.17) | copy-start | bytes 49156
  216.6 190.2 %all-to-all-start.1 = ((bf16[32,8,16,2048]{3,2,0,1:T(8,128)(2,1)}), bf16[32,8,16,2048]{3,2,0,1:T(8,128)(2,1)}, u32[]{:S(2)}, u32[]{:S(2)}) async-start(bf16[32,8,16,2048]{3,2,0,1:T(8,128)(2,1)} %copy.22), calls=%async_computation.1 | async-start | bytes 33554432 | tf_op jit(solution)/shard_map/all_to_all | solution.py:64
  223.3 2.9 copy-start.8
  224.0 2.2 copy-start.1
  226.3 2.5 copy-start.7
  272.5 177.9 %collective-permute-start = (bf16[4,64,2048]{2,1,0:T(8,128)(2,1)}, bf16[4,64,2048]{2,1,0:T(8,128)(2,1)S(1)}, u32[]{:S(2)}, u32[]{:S(2)}) collective-permute-start(bf16[4,64,2048]{2,1,0:T(8,128)(2,1)} %fusion.30), channel_id=1, source_target_pairs={{0,8},{8,16},{16,24},{24,0},{1,9},{9,17},{17,25},{25,1},{2,10},{10... | collective-permute-start | bytes 3145736 | tf_op jit(solution)/shard_map/ppermute | solution.py:73
  448.9 26.7 %copy-start.9 = (f32[1,2048]{1,0:T(1,128)S(1)}, f32[1,2048]{1,0:T(1,128)}, u32[]{:S(2)}) copy-start(f32[1,2048]{1,0:T(1,128)} %param.23) | copy-start | bytes 24580
  448.9 26.4 %collective-permute-start.1 = (bf16[4,64,2048]{2,1,0:T(8,128)(2,1)}, bf16[4,64,2048]{2,1,0:T(8,128)(2,1)S(1)}, u32[]{:S(2)}, u32[]{:S(2)}) collective-permute-start(bf16[4,64,2048]{2,1,0:T(8,128)(2,1)} %fusion.33), channel_id=1, source_target_pairs={{0,8},{8,16},{16,24},{24,0},{1,9},{9,17},{17,25},{25,1},{2,10},{10... | collective-permute-start | bytes 3145736 | tf_op jit(solution)/shard_map/ppermute | solution.py:73
  475.3 19.0 %copy-start.2 = (bf16[4,64,2048]{2,1,0:T(8,128)(2,1)}, bf16[4,64,2048]{2,1,0:T(8,128)(2,1)S(1)}, u32[]{:S(2)}) copy-start(bf16[4,64,2048]{2,1,0:T(8,128)(2,1)S(1)} %collective-permute-done.1) | copy-start | bytes 3145732
  475.6 15.3 %slice-start = ((s8[8388608]{0:T(1024)(128)(4,1)}), s8[4194304]{0:T(1024)(128)(4,1)S(1)}, s32[]{:S(2)}) async-start(s8[8388608]{0:T(1024)(128)(4,1)} %bitcast.186), calls=%async_computation.2 | async-start | bytes 8388608
  483.3 7.6 %slice-start.1 = ((s8[8388608]{0:T(1024)(128)(4,1)}), s8[4194304]{0:T(1024)(128)(4,1)S(1)}, s32[]{:S(2)}) async-start(s8[8388608]{0:T(1024)(128)(4,1)} %bitcast.186), calls=%async_computation.3 | async-start | bytes 8388608
  526.2 8.6 %copy-start.3 = (bf16[1,4,64,2048]{3,2,1,0:T(8,128)(2,1)S(1)}, bf16[1,4,64,2048]{3,2,1,0:T(8,128)(2,1)}, u32[]{:S(2)}) copy-start(bf16[1,4,64,2048]{3,2,1,0:T(8,128)(2,1)} %fusion.59) | copy-start | bytes 3145732
where the time goes:
time: 544 us; the launch traced here: 538 us
  waiting for transfers between devices  327 us (60%)
  local copies, waits for them, and re-layouts  92.7 us (17%)
  matrix products  68.3 us (13%)
  other arithmetic  32.2 us (6%)
  starting transfers between devices  17 us (3%)
    all_to_all x2, waiting for transfers between devices, device_step(): received = lax.all_to_all(local_out, 'ep', 1, 0, tiled=True)  302 us
    gather x2, local copies, waits for them, and re-layouts, gather_combine(): picked = jnp.take(row_table, row_ids, axis=0, mode='clip')  49.1 us
    ppermute x2, waiting for transfers between devices, device_step(): incoming = lax.ppermute(combined, 'pp', shift_pairs)  24.7 us
    reduce_sum x2, other arithmetic, gather_combine(): return jnp.sum(picked.astype(jnp.float32) * weights[..., None], axis=-2)  24.5 us
    another operation x2, local copies, waits for them, and re-layouts, device_step(): expert_out[0, micro_idx]  21 us
    slice x1, local copies, waits for them, and re-layouts, device_step(): expert_out[0, micro_idx]  18.6 us
    dot_general x2, matrix products, attention_block(): jnp.einsum('bqhe,bkhe->bhqk', queries, key_heads, preferred_element_type=...  17.7 us
    dot_general x2, matrix products, attention_block(): jnp.einsum('cirf,ife->cre', attn_mixed.astype(jnp.bfloat16), w_out, prefe...  17 us
  transfers between devices with their start and end apart: 4, of which 3 were waited for; matrix products, arithmetic and copies ran while one was open for 20% of the time, Pallas kernels for 0%

commit v1 on v0

v1 whole, which is shorter than its diff:
```python
import functools
import math
import jax
import jax.numpy as jnp
from jax import lax
from jax.experimental import pallas as pl
from jax.experimental.pallas import tpu as pltpu
from jax.sharding import PartitionSpec as P

EPSILON = 1e-6
CORES = 2
MESH = pl.DeviceIdType.MESH
BF16_MAX = 3.3895313892515355e38


def rms_norm(tensor, gain):
    values = tensor.astype(jnp.float32)
    inv_rms = lax.rsqrt(jnp.mean(values * values, axis=-1, keepdims=True) + EPSILON)
    return values * inv_rms * gain


def shared_expert(residual, norm_moe, w_gate, w_up, w_down):
    normed = rms_norm(residual, norm_moe).astype(jnp.bfloat16)
    gate_act = jnp.einsum("bld,df->blf", normed, w_gate, preferred_element_type=jnp.float32)
    up_act = jnp.einsum("bld,df->blf", normed, w_up, preferred_element_type=jnp.float32)
    hidden = (jax.nn.silu(gate_act) * up_act).astype(jnp.bfloat16)
    return jnp.einsum("blf,fd->bld", hidden, w_down, preferred_element_type=jnp.float32).astype(jnp.bfloat16)


def attention_block(combined, norm_attn, w_query, w_key, w_value, w_out):
    seq_len = combined.shape[1]
    score_scale = 1.0 / math.sqrt(w_query.shape[2])
    normed = rms_norm(combined, norm_attn).astype(jnp.bfloat16)
    queries = jnp.einsum("bld,dhe->blhe", normed, w_query, preferred_element_type=jnp.float32).astype(jnp.bfloat16)
    key_heads = jnp.einsum("bld,dhe->blhe", normed, w_key, preferred_element_type=jnp.float32).astype(jnp.bfloat16)
    value_heads = jnp.einsum("bld,dhe->blhe", normed, w_value, preferred_element_type=jnp.float32).astype(jnp.bfloat16)
    scores = jnp.einsum("bqhe,bkhe->bhqk", queries, key_heads, preferred_element_type=jnp.float32) * score_scale
    causal = jnp.arange(seq_len)[:, None] >= jnp.arange(seq_len)[None, :]
    scores = jnp.where(causal, scores, -1e30)
    attn_probs = jnp.exp(scores - jnp.max(scores, axis=-1, keepdims=True))
    prob_sum = jnp.sum(attn_probs, axis=-1, keepdims=True)
    attn_mixed = jnp.einsum("bhqk,bkhe->bhqe", attn_probs.astype(jnp.bfloat16), value_heads, preferred_element_type=jnp.float32) / prob_sum
    attn_proj = jnp.einsum("cirf,ife->cre", attn_mixed.astype(jnp.bfloat16), w_out, preferred_element_type=jnp.float32).astype(jnp.bfloat16)
    return (combined.astype(jnp.float32) + attn_proj.astype(jnp.float32)).astype(jnp.bfloat16)


def combine_kernel(stages, ep_size, eo, key, gate, resid, shared, y_out,
                   t_in, t_own, w, sbuf, pbuf, rbuf, rx, ysend,
                   tab_send, tab_recv, own_sem, ring_send, ring_recv, rx_send, rx_recv, y_send, y_recv):
    micros, experts, slots_total, dim = eo.shape
    chips = ep_size // CORES
    cap = slots_total // ep_size
    half = dim // CORES
    tok = key.shape[2]
    top_k = key.shape[3]
    rows = experts * cap
    group = tok // 2

    me = lax.axis_index("ep")
    pp = lax.axis_index("pp")
    chip, core = me // CORES, me % CORES
    other = 1 - core
    partner = chip * CORES + other
    step_mine = 1 + core * (chips - 2)
    step_other = 1 + other * (chips - 2)
    nxt = ((chip + step_mine) % chips) * CORES + core
    prv = ((chip + chips - step_mine) % chips) * CORES + core
    up = (pp + 1) % stages
    down = (pp + stages - 1) % stages

    barrier = pltpu.get_barrier_semaphore()
    pl.semaphore_signal(barrier, inc=1, device_id={"ep": prv}, device_id_type=MESH)
    pl.semaphore_signal(barrier, inc=1, device_id={"ep": partner}, device_id_type=MESH)
    pl.semaphore_signal(barrier, inc=1, device_id={"pp": down}, device_id_type=MESH)
    pl.semaphore_wait(barrier, 3)

    def dest_chip(s, stride):
        return (chip + (chips - s) * stride) % chips

    def cols(which):
        return pl.ds(pl.multiple_of(which * half, 128), half)

    def table_copy(micro, s, j):
        dest = dest_chip(s, step_other) * CORES + (other + j) % CORES
        return pltpu.make_async_remote_copy(
            src_ref=eo.at[micro, :, pl.ds(pl.multiple_of(dest * cap, 16), cap), cols(other)],
            dst_ref=t_in.at[micro, s - 1, j],
            send_sem=tab_send.at[micro, s - 1, j],
            recv_sem=tab_recv.at[micro, s - 1, j],
            device_id={"ep": partner}, device_id_type=MESH)

    def own_copy(micro, s, j, slot):
        dest = dest_chip(s, step_mine) * CORES + (core + j) % CORES
        return pltpu.make_async_copy(
            eo.at[micro, :, pl.ds(pl.multiple_of(dest * cap, 16), cap), cols(core)],
            t_own.at[slot, j], own_sem.at[slot, j])

    units = [(m, s) for m in range(micros) for s in range(1, chips + 1)]
    for m, s in units:
        for j in range(CORES):
            table_copy(m, s, j).start()

    def load_own(u):
        m, s = units[u]
        for j in range(CORES):
            own_copy(m, s, j, u % 2).start()

    load_own(0)
    load_own(1)

    block = 16

    def partial(u, out):
        m, s = units[u]
        for j in range(CORES):
            dest = dest_chip(s, step_mine) * CORES + (core + j) % CORES

            def build(b, _):
                r0 = pl.multiple_of(b * block, block)
                keys = key[m, dest, pl.ds(r0, block), :]
                gates = gate[m, dest, pl.ds(r0, block), :]
                lane = lax.broadcasted_iota(jnp.int32, (block, rows), 1)
                for h, holder in enumerate((me, partner)):
                    local = keys - holder * rows
                    weights = jnp.zeros((block, rows), jnp.float32)
                    for choice in range(top_k):
                        weights = jnp.where(local[:, choice:choice + 1] == lane, gates[:, choice:choice + 1], weights)
                    high = jnp.minimum(weights, BF16_MAX).astype(jnp.bfloat16)
                    rest = weights - high.astype(jnp.float32)
                    mid = rest.astype(jnp.bfloat16)
                    low = (rest - mid.astype(jnp.float32)).astype(jnp.bfloat16)
                    w[h, 0, pl.ds(r0, block), :] = high
                    w[h, 1, pl.ds(r0, block), :] = mid
                    w[h, 2, pl.ds(r0, block), :] = low
                return 0

            lax.fori_loop(0, tok // block, build, 0)
            own_copy(m, s, j, u % 2).wait()
            table_copy(m, s, j).wait_recv()

            def mult(n, _):
                c0 = pl.multiple_of(n * 256, 256)
                acc = jnp.zeros((tok, 256), jnp.float32)
                for h in range(2):
                    table = t_own.at[u % 2, j] if h == 0 else t_in.at[m, s - 1, j]
                    block_rows = table[:, :, pl.ds(c0, 256)].reshape(rows, 256)
                    for part in range(3):
                        acc += jnp.dot(w[h, part], block_rows, preferred_element_type=jnp.float32)
                for grp in range(2):
                    out[grp, j, :, pl.ds(c0, 256)] = acc[grp * group:(grp + 1) * group]
                return 0

            lax.fori_loop(0, half // 256, mult, 0)
        if u + 2 < len(units):
            load_own(u + 2)

    def ring_copy(m, s, grp):
        src = sbuf.at[m, grp] if s == 1 else rbuf.at[m, s - 2, grp]
        return pltpu.make_async_remote_copy(
            src_ref=src, dst_ref=rbuf.at[m, s - 1, grp],
            send_sem=ring_send.at[m, s - 1, grp], recv_sem=ring_recv.at[m, s - 1, grp],
            device_id={"ep": nxt}, device_id_type=MESH)

    def add_in(m, s, grp, slot):
        def body(b, _):
            r0 = pl.multiple_of(b * 8, 8)
            for j in range(CORES):
                rbuf[m, s - 1, grp, j, pl.ds(r0, 8), :] += pbuf[slot, grp, j, pl.ds(r0, 8), :]
            return 0
        lax.fori_loop(0, group // 8, body, 0)

    def pass_on(m, s, slot):
        for grp in range(2):
            ring_copy(m, s, grp).wait_recv()
            add_in(m, s, grp, slot)
            ring_copy(m, s + 1, grp).start()

    def rx_copy(m, grp):
        return pltpu.make_async_remote_copy(
            src_ref=rbuf.at[m, chips - 2, grp, 1], dst_ref=rx.at[m, grp],
            send_sem=rx_send.at[m, grp], recv_sem=rx_recv.at[m, grp],
            device_id={"ep": partner}, device_id_type=MESH)

    def y_copy(m, grp):
        return pltpu.make_async_remote_copy(
            src_ref=ysend.at[m, grp], dst_ref=y_out.at[m, grp],
            send_sem=y_send.at[m, grp], recv_sem=y_recv.at[m, grp],
            device_id={"pp": up}, device_id_type=MESH)

    def finish(m, slot):
        for grp in range(2):
            ring_copy(m, chips - 1, grp).wait_recv()
            add_in(m, chips - 1, grp, slot)
            rx_copy(m, grp).start()
        for grp in range(2):
            rx_copy(m, grp).wait_recv()

            def body(b, _):
                r0 = pl.multiple_of(b * 16, 16)
                for which, sums in ((core, rbuf.at[m, chips - 2, grp, 0]), (other, rx.at[m, grp])):
                    base = resid[m, grp, pl.ds(r0, 16), cols(which)].astype(jnp.float32)
                    base = base + shared[m, grp, pl.ds(r0, 16), cols(which)].astype(jnp.float32)
                    ysend[m, grp, pl.ds(r0, 16), cols(which)] = (base + sums[pl.ds(r0, 16), :]).astype(jnp.bfloat16)
                return 0

            lax.fori_loop(0, group // 16, body, 0)
            y_copy(m, grp).start()

    def send_first(m):
        for grp in range(2):
            ring_copy(m, 1, grp).start()

    partial(0, sbuf.at[0])
    send_first(0)
    partial(1, pbuf.at[0])
    partial(2, pbuf.at[1])
    pass_on(0, 1, 0)
    partial(3, pbuf.at[0])
    partial(4, sbuf.at[1])
    pass_on(0, 2, 1)
    send_first(1)
    partial(5, pbuf.at[1])
    finish(0, 0)
    partial(6, pbuf.at[0])
    pass_on(1, 1, 1)
    partial(7, pbuf.at[1])
    pass_on(1, 2, 0)
    finish(1, 1)

    for m, s in units:
        for j in range(CORES):
            table_copy(m, s, j).wait_send()
    for m in range(micros):
        for grp in range(2):
            for s in range(1, chips):
                ring_copy(m, s, grp).wait_send()
            rx_copy(m, grp).wait_send()
            y_copy(m, grp).wait()


def solution(mesh):
    stages = mesh.shape["pp"]
    ep_size = mesh.shape["ep"]
    tok_spec = P("pp", "data", "ep", None, None)
    vec_spec = P("pp", None)
    mat_spec = P("pp", None, None)
    head_spec = P("pp", None, None, None)

    def device_step(expert_out, expert_ids, slot_ids, gate_weights, residual, norm_moe, w_gate, w_up, w_down, norm_attn, w_query, w_key, w_value, w_out):
        micros, experts, slots_total, dim = expert_out.shape[1:]
        cap = slots_total // ep_size
        chips = ep_size // CORES
        half = dim // CORES
        seqs, seq_len, top_k = expert_ids.shape[2:]
        tok = seqs * seq_len
        group = tok // 2
        first_slot = lax.axis_index("ep") * cap
        slot_here = slot_ids[0].reshape(micros, tok, top_k)
        key = jnp.where(slot_here >= 0, expert_ids[0].reshape(micros, tok, top_k) * cap + slot_here - first_slot, -1)
        key = lax.all_gather(key, "ep", axis=1)
        gate = lax.all_gather(gate_weights[0].reshape(micros, tok, top_k), "ep", axis=1)
        resid = residual[0].reshape(micros * seqs, seq_len, dim)
        shared = shared_expert(resid, norm_moe[0], w_gate[0], w_up[0], w_down[0])
        vmem = pl.BlockSpec(memory_space=pltpu.VMEM)
        anyspace = pl.BlockSpec(memory_space=pl.ANY)
        incoming = pl.pallas_call(
            functools.partial(combine_kernel, stages, ep_size),
            out_shape=jax.ShapeDtypeStruct((micros, 2, group, dim), jnp.bfloat16),
            in_specs=[anyspace, vmem, vmem, vmem, vmem],
            out_specs=anyspace,
            scratch_shapes=[
                pltpu.VMEM((micros, chips, CORES, experts, cap, half), jnp.bfloat16),
                pltpu.VMEM((2, CORES, experts, cap, half), jnp.bfloat16),
                pltpu.VMEM((2, 3, tok, experts * cap), jnp.bfloat16),
                pltpu.VMEM((micros, 2, CORES, group, half), jnp.float32),
                pltpu.VMEM((2, 2, CORES, group, half), jnp.float32),
                pltpu.VMEM((micros, chips - 1, 2, CORES, group, half), jnp.float32),
                pltpu.VMEM((micros, 2, group, half), jnp.float32),
                pltpu.VMEM((micros, 2, group, dim), jnp.bfloat16),
                pltpu.SemaphoreType.DMA((micros, chips, CORES)),
                pltpu.SemaphoreType.DMA((micros, chips, CORES)),
                pltpu.SemaphoreType.DMA((2, CORES)),
                pltpu.SemaphoreType.DMA((micros, chips - 1, 2)),
                pltpu.SemaphoreType.DMA((micros, chips - 1, 2)),
                pltpu.SemaphoreType.DMA((micros, 2)),
                pltpu.SemaphoreType.DMA((micros, 2)),
                pltpu.SemaphoreType.DMA((micros, 2)),
                pltpu.SemaphoreType.DMA((micros, 2)),
            ],
            compiler_params=pltpu.CompilerParams(collective_id=0, has_side_effects=True, vmem_limit_bytes=66_000_000),
            cost_estimate=pl.CostEstimate(flops=30_000_000_000, bytes_accessed=64_000_000, transcendentals=0),
        )(expert_out[0], key, gate, residual[0].reshape(micros, 2, group, dim), shared.reshape(micros, 2, group, dim))
        out = attention_block(incoming.reshape(micros * seqs, seq_len, dim), norm_attn[0], w_query[0], w_key[0], w_value[0], w_out[0])
        return out.reshape(1, micros, seqs, seq_len, dim)

    in_specs = (tok_spec,) * 5 + (vec_spec, mat_spec, mat_spec, mat_spec, vec_spec, head_spec, head_spec, head_spec, head_spec)
    return jax.shard_map(device_step, mesh=mesh, in_specs=in_specs, out_specs=tok_spec, check_vma=False)
```

time: 544 us -> 292 us (0.54)
  waiting for transfers between devices: 327 us -> 0 us
  Pallas kernels: 0 us -> 182 us
  local copies, waits for them, and re-layouts: 92.7 us -> 6.02 us
  blocking collectives: 0 us -> 52.1 us
  matrix products: 68.3 us -> 42.9 us
  other arithmetic: 32.2 us -> 6.82 us
  starting transfers between devices: 17 us -> 0 us
    all_to_all x2 -> x0, waiting for transfers between devices: 302 us -> none  [device_step(): received = lax.all_to_all(local_out, 'ep', 1, 0, tiled=True)]
    pallas_call x0 -> x1, Pallas kernels: none -> 182 us  [device_step(): pl.pallas_call(functools.partial(combine_kernel, stages, ep_size), out_sh...]
    all_gather x0 -> x2, blocking collectives: none -> 52.1 us  [the longest x1 27.6 us: device_step(): key = lax.all_gather(key, 'ep', axis=1)]
    gather x2 -> x0, local copies, waits for them, and re-layouts: 49.1 us -> none  [gather_combine(): picked = jnp.take(row_table, row_ids, axis=0, mode='clip')]
    ppermute x2 -> x0, waiting for transfers between devices: 24.7 us -> none  [device_step(): incoming = lax.ppermute(combined, 'pp', shift_pairs)]
    reduce_sum x2 -> x0, other arithmetic: 24.5 us -> none  [gather_combine(): return jnp.sum(picked.astype(jnp.float32) * weights[..., None], axis=-2)]
    another operation x2 -> x0, local copies, waits for them, and re-layouts: 21 us -> none  [device_step(): expert_out[0, micro_idx]]
    slice x1 -> x0, local copies, waits for them, and re-layouts: 18.6 us -> none  [device_step(): expert_out[0, micro_idx]]
  transfers between devices with their start and end apart: 4 -> 0, of which waited for: 3 -> 0; matrix products, arithmetic and copies ran while one was open for 20% -> 0% of each run, Pallas kernels for 0% -> 0%
where the time goes in v1:
time: 292 us; the launch traced here: 290 us
  Pallas kernels  182 us (62%)
  blocking collectives  52.1 us (18%)
  matrix products  42.9 us (15%)
  other arithmetic  6.82 us (2%)
  local copies, waits for them, and re-layouts  6.02 us (2%)
    pallas_call x1, Pallas kernels, device_step(): pl.pallas_call(functools.partial(combine_kernel, stages, ep_size), out_sh...  182 us
    all_gather x1, blocking collectives, device_step(): key = lax.all_gather(key, 'ep', axis=1)  27.6 us
    all_gather x1, blocking collectives, device_step(): lax.all_gather(gate_weights[0].reshape(micros, tok, top_k), 'ep', axis=1)  24.5 us
    dot_general x1, matrix products, attention_block(): jnp.einsum('cirf,ife->cre', attn_mixed.astype(jnp.bfloat16), w_out, prefe...  11.4 us
    dot_general x1, matrix products, attention_block(): jnp.einsum('bld,dhe->blhe', normed, w_value, preferred_element_type=jnp.f...  8.8 us
    dot_general x1, matrix products, attention_block(): jnp.einsum('bld,dhe->blhe', normed, w_query, preferred_element_type=jnp.f...  6.57 us
    dot_general x1, matrix products, shared_expert(): jnp.einsum('blf,fd->bld', hidden, w_down, preferred_element_type=jnp.floa...  6.35 us
    dot_general x1, matrix products, attention_block(): jnp.einsum('bld,dhe->blhe', normed, w_key, preferred_element_type=jnp.flo...  6.31 us

profile of v1, /device:TPU:97, one launch (start us, length us, event | category | flops | bytes accessed | tf_op | source)
XLA Modules:
  0.0 290.3 jit_solution(16622766463960075006)
XLA Ops:
  0.0 0.0 copy-start.5
  0.0 0.0 copy-start.3
  0.0 0.0 copy-start.4
  0.0 2.1 fusion.8
  2.1 0.0 copy-done.3
  2.2 0.0 copy-done.4
  2.2 0.1 copy.15
  2.3 0.0 copy-done.5
  2.3 0.1 copy.16
  2.5 0.0 copy-start.1
  2.5 0.0 copy-start.6
  2.5 24.5 %all_gather.8.gate = f32[2,8,256,8]{3,2,1,0:T(8,128)} all-gather(f32[2,1,256,8]{3,2,1,0:T(8,128)S(1)} %bitcast.68), channel_id=1, replica_groups=mesh['data'=1,'pp'=4,'ep'=8] {'ep'}, dimensions={1}, use_global_device_ids=true | all-gather | bytes 147456 | tf_op jit(solution)/shard_map/all_gather | solution.py:261
  27.0 27.6 %all_gather.7.key = s32[2,8,256,8]{3,2,1,0:T(8,128)} all-gather(s32[2,1,256,8]{3,2,1,0:T(8,128)S(1)} %bitcast.67), channel_id=1, replica_groups=mesh['data'=1,'pp'=4,'ep'=8] {'ep'}, dimensions={1}, use_global_device_ids=true | all-gather | bytes 147456 | tf_op jit(solution)/shard_map/all_gather | solution.py:260
  54.6 0.0 copy-done.1
  54.6 0.0 copy-done.6
  54.6 0.0 copy-start.8
  54.6 0.5 fusion.10
  55.2 1.0 copy-done.8
  56.2 2.2 fusion.27
  58.4 6.3 %convolution_convert_fusion = bf16[8,64,2048]{2,1,0:T(8,128)(2,1)} fusion(bf16[1,512,2048]{2,1,0:T(8,128)(2,1)} %param.22, bf16[8,64,2048]{2,1,0:T(8,128)(2,1)S(1)} %bitcast.63, bf16[1,2048,512]{2,1,0:T(8,128)(2,1)} %param.21, f32[8,64,512]{2,1,0:T(8,128)} %fusion.27), kind=kOutput, calls=%fused_computation.24 | convolution fusion | flops 2150105088 | bytes 9437184 | tf_op jit(solution)/shard_map/blf,fd->bld/dot_general | solution.py:27
  64.8 0.0 copy-start.7
  64.8 182.2 %shard_map.136 = bf16[2,2,128,2048]{3,2,1,0:T(8,128)(2,1)} custom-call(bf16[2,32,128,2048]{3,2,1,0:T(8,128)(2,1)} %bitcast.71, s32[2,8,256,8]{3,2,1,0:T(8,128)} %all_gather.7.key, f32[2,8,256,8]{3,2,1,0:T(8,128)} %all_gather.8.gate, bf16[2,2,128,2048]{3,2,1,0:T(8,128)(2,1)} %bitcast.60, bf16[2,2,128,2048]{3,2,1,0:T(8,128)(2,1)} %bitcast.79), custom_call_target="tpu_custom_call" | custom-call | flops 30000001024 | bytes 64000000 | tf_op jit(solution)/shard_map/pallas_call | solution.py:266
  247.0 0.0 copy-start.2
  247.0 2.2 multiply_reduce_fusion
  249.2 0.0 copy-done.7
  249.2 0.0 copy-done.2
  249.2 0.0 slice-start
  249.3 0.5 multiply_convert_fusion
  249.8 0.0 slice-start.1
  249.8 8.8 %fusion.2 = bf16[8,64,16,128]{3,1,2,0:T(8,128)(2,1)S(1)} fusion(bf16[8,64,2048,1]{2,1,3,0:T(8,128)(2,1)S(1)} %bitcast.64, bf16[2048,16,128,1]{2,1,0,3:T(8,128)(2,1)} %bitcast.72), kind=kOutput, calls=%fused_computation.2 | convolution fusion | flops 4294967296 | bytes 12582912 | tf_op jit(solution)/shard_map/bld,dhe->blhe/dot_general | solution.py:36
  258.6 0.0 slice-start.2
  258.6 2.7 copy.34
  261.4 0.0 slice-done
  261.4 0.0 slice-done.1
  261.4 0.0 slice-start.3
  261.4 6.3 %fusion.4 = bf16[8,64,16,128]{3,1,2,0:T(8,128)(2,1)S(1)} fusion(bf16[8,64,2048,1]{2,1,3,0:T(8,128)(2,1)S(1)} %bitcast.65, bf16[2048,16,128,1]{2,1,0,3:T(8,128)(2,1)S(1)} %bitcast.75), kind=kOutput, calls=%fused_computation.4 | convolution fusion | flops 4294967296 | bytes 12582912 | tf_op jit(solution)/shard_map/bld,dhe->blhe/dot_general | solution.py:35
  267.7 0.0 slice-done.2
  267.7 0.0 slice-done.3
  267.7 6.6 %fusion.6 = bf16[8,64,16,128]{3,1,2,0:T(8,128)(2,1)S(1)} fusion(bf16[8,64,2048,1]{2,1,3,0:T(8,128)(2,1)S(1)} %bitcast.66, bf16[2048,16,128,1]{2,1,0,3:T(8,128)(2,1)S(1)} %bitcast.78), kind=kOutput, calls=%fused_computation.6 | convolution fusion | flops 4294967296 | bytes 12582912 | tf_op jit(solution)/shard_map/bld,dhe->blhe/dot_general | solution.py:34
  274.3 1.3 fusion.11
  275.6 0.0 copy-start
  275.6 1.9 copy-done
  277.5 1.4 fusion.14
  278.9 11.4 %add_convert_fusion = bf16[8,64,2048]{2,1,0:T(8,128)(2,1)} fusion(bf16[1,16,128,2048]{3,2,1,0:T(8,128)(2,1)} %param.27, f32[8,16,64,64]{2,3,1,0:T(8,128)} %copy-done, bf16[8,64,16,128]{3,2,1,0:T(8,128)(2,1)} %copy.34, f32[8,16,64]{2,1,0:T(8,128)S(1)} %fusion.14, f32[8,16,64]{2,1,0:T(8,128)S(1)} %get-tuple-element.5, ...), kind=kOutput, calls=%fused_computation.15 | convolution fusion | flops 4438622208 | bytes 16846848 | tf_op jit(solution)/shard_map/cirf,ife->cre/dot_general | solution.py:43
  (6 shorter events, 0.0 us)
Async XLA Ops:
  0.0 2.3 copy-start.5
  0.0 2.1 copy-start.3
  0.0 2.2 copy-start.4
  2.5 52.1 %copy-start.1 = (bf16[1,2,4,64,2048]{4,3,2,1,0:T(8,128)(2,1)S(1)}, bf16[1,2,4,64,2048]{4,3,2,1,0:T(8,128)(2,1)}, u32[]{:S(2)}) copy-start(bf16[1,2,4,64,2048]{4,3,2,1,0:T(8,128)(2,1)} %param.18) | copy-start | bytes 6291460
  2.5 52.1 %copy-start.6 = (f32[1,2048]{1,0:T(1,128)S(1)}, f32[1,2048]{1,0:T(1,128)}, u32[]{:S(2)}) copy-start(f32[1,2048]{1,0:T(1,128)} %param.19) | copy-start | bytes 24580
  54.6 1.6 copy-start.8
  64.8 184.5 %copy-start.7 = (f32[1,2048]{1,0:T(1,128)S(1)}, f32[1,2048]{1,0:T(1,128)}, u32[]{:S(2)}) copy-start(f32[1,2048]{1,0:T(1,128)} %param.23) | copy-start | bytes 24580
  247.0 2.3 copy-start.2
  249.2 12.1 %slice-start = ((s8[8388608]{0:T(1024)(128)(4,1)}), s8[4194304]{0:T(1024)(128)(4,1)S(1)}, s32[]{:S(2)}) async-start(s8[8388608]{0:T(1024)(128)(4,1)} %bitcast.73), calls=%async_computation | async-start | bytes 8388608
  249.8 11.6 %slice-start.1 = ((s8[8388608]{0:T(1024)(128)(4,1)}), s8[4194304]{0:T(1024)(128)(4,1)S(1)}, s32[]{:S(2)}) async-start(s8[8388608]{0:T(1024)(128)(4,1)} %bitcast.73), calls=%async_computation.1 | async-start | bytes 8388608
  258.6 9.1 %slice-start.2 = ((s8[8388608]{0:T(1024)(128)(4,1)}), s8[4194304]{0:T(1024)(128)(4,1)S(1)}, s32[]{:S(2)}) async-start(s8[8388608]{0:T(1024)(128)(4,1)} %bitcast.76), calls=%async_computation.2 | async-start | bytes 8388608
  261.4 6.3 %slice-start.3 = ((s8[8388608]{0:T(1024)(128)(4,1)}), s8[4194304]{0:T(1024)(128)(4,1)S(1)}, s32[]{:S(2)}) async-start(s8[8388608]{0:T(1024)(128)(4,1)} %bitcast.76), calls=%async_computation.3 | async-start | bytes 8388608
  275.6 1.9 copy-start

commit v2 on v0

v2 whole, which is shorter than its diff:
```python
import functools
import math
import jax
import jax.numpy as jnp
from jax import lax
from jax.experimental import pallas as pl
from jax.experimental.pallas import tpu as pltpu
from jax.sharding import PartitionSpec as P

EPSILON = 1e-6
CORES = 2
PARTS = 3
GROUPS = 2
MESH = pl.DeviceIdType.MESH
BF16_MAX = 3.3895313892515355e38
F32 = jnp.float32
BF16 = jnp.bfloat16


def dot(a, b):
    return jnp.dot(a, b, preferred_element_type=F32)


def boundary_kernel(stages, ep_size, seq_len,
                    eo, ids, slots, gates, resid, norm_moe, w_gate, w_up, w_down, norm_attn, w_query, w_key, w_value, w_out,
                    out, w_heads,
                    t_in, t_own, w, sbuf, pbuf, rbuf, rx, ysend, y_in, shared, pool_in, pool_out, raw, turned, xn, acc, kp, kr, kt,
                    tab_send, tab_recv, own_sem, ring_send, ring_recv, rx_send, rx_recv, y_send, y_recv,
                    key_send, key_recv, load_sem, raw_sem, turn_sem, out_sem, free_sem):
    micros, experts, slots_total, dim = eo.shape
    chips = ep_size // CORES
    cap = slots_total // ep_size
    half = dim // CORES
    top_k = ids.shape[2]
    group = rbuf.shape[4]
    tok = group * GROUPS
    seqs = group // seq_len
    rows = experts * cap
    heads, head_dim = w_query.shape[1:]
    head_groups, width = w_heads.shape[1], w_heads.shape[3]
    ff = w_gate.shape[1]

    me = lax.axis_index("ep")
    pp = lax.axis_index("pp")
    chip, core = me // CORES, me % CORES
    other = 1 - core
    partner = chip * CORES + other
    step_mine = 1 + core * (chips - 2)
    step_other = 1 + other * (chips - 2)
    nxt = ((chip + step_mine) % chips) * CORES + core
    up = (pp + 1) % stages
    down = (pp + stages - 1) % stages

    peers = [(a, b) for a in range(chips) for b in range(CORES) if (a, b) != (0, 0)]

    def peer_id(a, b):
        return ((chip + a) % chips) * CORES + (core + b) % CORES

    barrier = pltpu.get_barrier_semaphore()
    for a, b in peers:
        pl.semaphore_signal(barrier, inc=1, device_id={"ep": peer_id(a, b)}, device_id_type=MESH)
    pl.semaphore_signal(barrier, inc=1, device_id={"pp": down}, device_id_type=MESH)

    def dest_chip(s, stride):
        return (chip + (chips - s) * stride) % chips

    def cols(which):
        return pl.ds(pl.multiple_of(which * half, 128), half)

    def table_copy(m, s, j):
        dest = dest_chip(s, step_other) * CORES + (other + j) % CORES
        return pltpu.make_async_remote_copy(
            src_ref=eo.at[m, :, pl.ds(pl.multiple_of(dest * cap, 16), cap), cols(other)],
            dst_ref=t_in.at[s - 1, j], send_sem=tab_send.at[m, s - 1, j], recv_sem=tab_recv.at[m, s - 1, j],
            device_id={"ep": partner}, device_id_type=MESH)

    units = [(m, s) for m in range(micros) for s in range(1, chips + 1)]

    def own_copy(u, j):
        m, s = units[u]
        dest = dest_chip(s, step_mine) * CORES + (core + j) % CORES
        return pltpu.make_async_copy(
            eo.at[m, :, pl.ds(pl.multiple_of(dest * cap, 16), cap), cols(core)],
            t_own.at[u % 2, j], own_sem.at[u % 2, j])

    def load_own(u):
        for j in range(CORES):
            own_copy(u, j).start()

    load_own(0)
    load_own(1)

    def shared_loads():
        halves = [pl.ds(0, width), pl.ds(width, width)]
        return [
            pltpu.make_async_copy(w_gate.at[:, halves[0]], pool_in.at[0, 0], load_sem.at[0, 0]),
            pltpu.make_async_copy(w_gate.at[:, halves[1]], pool_in.at[0, 1], load_sem.at[0, 1]),
            pltpu.make_async_copy(w_up.at[:, halves[0]], pool_in.at[0, 2], load_sem.at[0, 2]),
            pltpu.make_async_copy(w_up.at[:, halves[1]], pool_in.at[1, 0], load_sem.at[1, 0]),
            pltpu.make_async_copy(w_down.at[halves[0]], pool_out.at[0], load_sem.at[0, 3]),
            pltpu.make_async_copy(w_down.at[halves[1]], pool_out.at[1], load_sem.at[1, 3]),
        ]

    first = me * cap
    for m in range(micros):
        for grp in range(GROUPS):
            key_rows, gate_rows = [], []
            for q in range(seqs):
                slot_here = slots[m, grp * seqs + q]
                key_here = ids[m, grp * seqs + q] * cap + (slot_here - first)
                key_rows.append(jnp.where(slot_here >= 0, key_here, -1).astype(F32))
                gate_rows.append(gates[m, grp * seqs + q])
            key_rows = jnp.concatenate(key_rows, axis=1)
            gate_rows = jnp.concatenate(gate_rows, axis=1)
            kp[m, grp, 0] = key_rows
            kp[m, grp, 1] = gate_rows
            kr[m, grp, (chips - 1) * CORES, 0] = key_rows
            kr[m, grp, (chips - 1) * CORES, 1] = gate_rows

    pl.semaphore_wait(barrier, len(peers) + 1)

    def key_copy(a, b):
        stride = 1 + ((core + b) % CORES) * (chips - 2)
        place = ((chips - 1 + a * stride) % chips) * CORES + b
        return pltpu.make_async_remote_copy(
            src_ref=kp, dst_ref=kr.at[:, :, place], send_sem=key_send.at[a, b], recv_sem=key_recv.at[place],
            device_id={"ep": peer_id(a, b)}, device_id_type=MESH)

    def key_arrival(place):
        return pltpu.make_async_remote_copy(
            src_ref=kp, dst_ref=kr.at[:, :, place], send_sem=key_send.at[0, 0], recv_sem=key_recv.at[place],
            device_id={"ep": partner}, device_id_type=MESH)

    for a, b in peers:
        key_copy(a, b).start()
    for s in range(1, chips + 1):
        for j in range(CORES):
            table_copy(0, s, j).start()
    for copy in shared_loads():
        copy.start()
    for place in range(chips * CORES):
        if place != (chips - 1) * CORES:
            key_arrival(place).wait_recv()
    for m in range(micros):
        for grp in range(GROUPS):
            kt[m, grp] = kr[m, grp].reshape(chips * CORES * 2 * top_k, group).T

    block = 32
    lane = lax.broadcasted_iota(jnp.int32, (block, rows), 1).astype(F32)

    def build_rows(v, grp, r0):
        m, s = units[v // CORES]
        base = ((s - 1) * CORES + v % CORES) * 2 * top_k
        known = kt[m, grp, pl.ds(r0, block), :]
        keys, scale = known[:, base:base + top_k], known[:, base + top_k:base + 2 * top_k]
        r1 = pl.multiple_of(grp * group + r0, block)
        for h, holder in enumerate((me, partner)):
            local = keys - (holder * rows).astype(F32)
            weights = jnp.zeros((block, rows), F32)
            for choice in range(top_k):
                weights = jnp.where(local[:, choice:choice + 1] == lane, scale[:, choice:choice + 1], weights)
            high = jnp.minimum(weights, BF16_MAX).astype(BF16)
            rest = weights - high.astype(F32)
            mid = rest.astype(BF16)
            low = (rest - mid.astype(F32)).astype(BF16)
            for part, value in enumerate((high, mid, low)):
                w[v % 2, h, part, pl.ds(r1, block), :] = value

    pieces = half // width

    def step(v, target):
        u, j = v // CORES, v % CORES
        m, s = units[u]
        own_copy(u, j).wait()
        table_copy(m, s, j).wait_recv()
        span = tok // pieces

        def body(n, _):
            c0 = pl.multiple_of(n * width, width)
            total = None
            for h in range(2):
                table = (t_own.at[u % 2, j] if h == 0 else t_in.at[s - 1, j])[:, :, pl.ds(c0, width)].reshape(rows, width)
                for part in range(PARTS):
                    term = dot(w[v % 2, h, part], table)
                    total = term if total is None else total + term
            for grp in range(GROUPS):
                target[grp, j, :, pl.ds(c0, width)] = total[grp * group:(grp + 1) * group]
            if v + 1 < len(units) * CORES:
                for b in range(span // block):
                    row = n * span + b * block
                    build_rows(v + 1, row // group, pl.multiple_of(row % group, block))
            return 0

        lax.fori_loop(0, pieces, body, 0)
        if j == CORES - 1:
            if u + 2 < len(units):
                load_own(u + 2)
            if m == 0:
                pl.semaphore_signal(free_sem.at[s - 1], inc=1, device_id={"ep": partner}, device_id_type=MESH)

    def next_tables(s):
        pl.semaphore_wait(free_sem.at[s - 1], 1)
        for j in range(CORES):
            table_copy(1, s, j).start()

    def ring_copy(m, s, grp, j, q):
        part = pl.ds(q * seq_len, seq_len)
        src = sbuf.at[grp, j, part] if s == 1 else rbuf.at[m, s - 2, grp, j, part]
        return pltpu.make_async_remote_copy(
            src_ref=src, dst_ref=rbuf.at[m, s - 1, grp, j, part],
            send_sem=ring_send.at[m, s - 1, grp, j, q], recv_sem=ring_recv.at[m, s - 1, grp, j, q],
            device_id={"ep": nxt}, device_id_type=MESH)

    def send_first(m, j):
        for grp in range(GROUPS):
            for q in range(seqs):
                ring_copy(m, 1, grp, j, q).start()

    def add_in(m, s, grp, j, q, slot):
        for b in range(seq_len // block):
            part = pl.ds(q * seq_len + b * block, block)
            rbuf[m, s - 1, grp, j, part, :] += pbuf[slot, grp, j, part, :]

    def rx_copy(m, grp, q):
        part = pl.ds(q * seq_len, seq_len)
        return pltpu.make_async_remote_copy(
            src_ref=rbuf.at[m, chips - 2, grp, 1, part], dst_ref=rx.at[m, grp, part],
            send_sem=rx_send.at[m, grp, q], recv_sem=rx_recv.at[m, grp, q],
            device_id={"ep": partner}, device_id_type=MESH)

    def arrive(m, s, grp, slot):
        for q in range(seqs):
            for j in (1, 0):
                ring_copy(m, s, grp, j, q).wait_recv()
                add_in(m, s, grp, j, q, slot)
                if s < chips - 1:
                    ring_copy(m, s + 1, grp, j, q).start()
                elif j == 1:
                    rx_copy(m, grp, q).start()

    def y_copy(m, grp, q):
        part = pl.ds(q * seq_len, seq_len)
        return pltpu.make_async_remote_copy(
            src_ref=ysend.at[grp, part], dst_ref=y_in.at[m, pl.ds(grp * group + q * seq_len, seq_len)],
            send_sem=y_send.at[m, grp, q], recv_sem=y_recv.at[m, grp, q],
            device_id={"pp": up}, device_id_type=MESH)

    def combine(m, grp):
        for q in range(seqs):
            if m > 0:
                y_copy(m - 1, grp, q).wait_send()
            rx_copy(m, grp, q).wait_recv()

            def body(b, _):
                r0 = pl.multiple_of(q * seq_len + b * 16, 16)
                r1 = pl.multiple_of(m * tok + grp * group + r0, 16)
                for which, sums in ((core, rbuf.at[m, chips - 2, grp, 0]), (other, rx.at[m, grp])):
                    base = resid[pl.ds(r1, 16), cols(which)].astype(F32) + shared[pl.ds(r1, 16), cols(which)].astype(F32)
                    ysend[grp, pl.ds(r0, 16), cols(which)] = (base + sums[pl.ds(r0, 16), :]).astype(BF16)
                return 0

            lax.fori_loop(0, seq_len // 16, body, 0)
            y_copy(m, grp, q).start()

    def normalize(source, base, count, gain):
        def body(b, _):
            r0 = pl.multiple_of(b * 16, 16)
            values = source[pl.ds(pl.multiple_of(base + r0, 16), 16), :].astype(F32)
            inv_rms = lax.rsqrt(jnp.mean(values * values, axis=-1, keepdims=True) + EPSILON)
            xn[pl.ds(r0, 16), :] = (values * inv_rms * gain[...]).astype(BF16)
            return 0
        lax.fori_loop(0, count // 16, body, 0)

    def shared_expert():
        for copy in shared_loads():
            copy.wait()
        gate_refs = (pool_in.at[0, 0], pool_in.at[0, 1])
        up_refs = (pool_in.at[0, 2], pool_in.at[1, 0])

        def body(m, _):
            normalize(resid, m * tok, tok, norm_moe)
            hidden = []
            for f in range(ff // width):
                gate_act = dot(xn[...], gate_refs[f][...])
                up_act = dot(xn[...], up_refs[f][...])
                hidden.append((gate_act * jax.nn.sigmoid(gate_act) * up_act).astype(BF16))
            r0 = pl.multiple_of(m * tok, 16)
            for n in range(dim // (2 * width)):
                span = pl.ds(n * 2 * width, 2 * width)
                total = dot(hidden[0], pool_out[0, :, span]) + dot(hidden[1], pool_out[1, :, span])
                shared[pl.ds(r0, tok), span] = total.astype(BF16)
            return 0

        lax.fori_loop(0, micros, body, 0)

    chunk = raw.shape[1]

    def to_head_groups(kind, source):
        count = dim // chunk

        def fetch(c):
            return pltpu.make_async_copy(source.at[pl.ds(pl.multiple_of(c * chunk, chunk), chunk)], raw.at[c % 2], raw_sem.at[c % 2])

        def flush(c):
            return pltpu.make_async_copy(turned.at[c % 2], w_heads.at[kind, :, pl.ds(pl.multiple_of(c * chunk, chunk), chunk)], turn_sem.at[c % 2])

        fetch(0).start()

        def body(c, _):
            @pl.when(c + 1 < count)
            def _():
                fetch(c + 1).start()
            fetch(c).wait()

            @pl.when(c >= 2)
            def _():
                flush(c - 2).wait()

            def turn(b, _):
                r0 = pl.multiple_of(b * 32, 32)
                value = jnp.swapaxes(raw[c % 2, pl.ds(r0, 32)], 0, 1)
                for h in range(heads):
                    place = (h * head_dim) % width
                    turned[c % 2, h * head_dim // width, pl.ds(r0, 32), place:place + head_dim] = value[h]
                return 0

            lax.fori_loop(0, chunk // 32, turn, 0)
            flush(c).start()
            return 0

        lax.fori_loop(0, count, body, 0)
        flush(count - 2).wait()
        flush(count - 1).wait()

    def weight_loads(g, slot):
        loads = [pltpu.make_async_copy(w_heads.at[kind, g], pool_in.at[slot, kind], load_sem.at[slot, kind]) for kind in range(3)]
        loads.append(pltpu.make_async_copy(w_out.at[pl.ds(pl.multiple_of(g * width, width), width)], pool_out.at[slot], load_sem.at[slot, 3]))
        return loads

    def prefetch():
        for g in range(2):
            for copy in weight_loads(g, g):
                copy.start()

    span_q = 128
    score_scale = 1.0 / math.sqrt(head_dim)

    def attend(g0, g1):
        row = lax.broadcasted_iota(jnp.int32, (span_q, span_q), 0)
        col = lax.broadcasted_iota(jnp.int32, (span_q, span_q), 1)
        visible = (row >= col) & (row // seq_len == col // seq_len)

        def body(g, _):
            slot = g % 2
            for copy in weight_loads(g, slot):
                copy.wait()
            queries = dot(xn[...], pool_in[slot, 0]).astype(BF16)
            key_heads = dot(xn[...], pool_in[slot, 1]).astype(BF16)
            value_heads = dot(xn[...], pool_in[slot, 2]).astype(BF16)
            mixed = []
            for r in range(tok // span_q):
                line = []
                for h in range(width // head_dim):
                    part = (slice(r * span_q, (r + 1) * span_q), slice(h * head_dim, (h + 1) * head_dim))
                    scores = lax.dot_general(queries[part], key_heads[part], (((1,), (1,)), ((), ())), preferred_element_type=F32) * score_scale
                    scores = jnp.where(visible, scores, -1e30)
                    probs = jnp.exp(scores - jnp.max(scores, axis=-1, keepdims=True))
                    total = jnp.sum(probs, axis=-1, keepdims=True)
                    line.append((dot(probs.astype(BF16), value_heads[part]) / total).astype(BF16))
                mixed.append(jnp.concatenate(line, axis=1))
            mixed = jnp.concatenate(mixed, axis=0)
            for n in range(dim // (2 * width)):
                span = pl.ds(n * 2 * width, 2 * width)
                acc[:, span] += dot(mixed, pool_out[slot, :, span])

            @pl.when(g + 2 < head_groups)
            def _():
                for copy in weight_loads(g + 2, slot):
                    copy.start()
            return 0

        lax.fori_loop(g0, g1, body, 0)

    def out_copy(m):
        return pltpu.make_async_copy(xn, out.at[m], out_sem.at[m])

    def begin_attention(m):
        for grp in range(GROUPS):
            for q in range(seqs):
                y_copy(m, grp, q).wait_recv()
        if m > 0:
            out_copy(m - 1).wait()
        normalize(y_in.at[m], 0, tok, norm_attn)

        def clear(b, _):
            acc[pl.ds(pl.multiple_of(b * 16, 16), 16), :] = jnp.zeros((16, dim), F32)
            return 0

        lax.fori_loop(0, tok // 16, clear, 0)

    def end_attention(m):
        def body(b, _):
            r0 = pl.multiple_of(b * 16, 16)
            proj = acc[pl.ds(r0, 16), :].astype(BF16).astype(F32)
            xn[pl.ds(r0, 16), :] = (y_in[m, pl.ds(r0, 16), :].astype(F32) + proj).astype(BF16)
            return 0
        lax.fori_loop(0, tok // 16, body, 0)
        out_copy(m).start()

    def first_rows(b, _):
        row = b * block
        build_rows(0, row // group, pl.multiple_of(row % group, block))
        return 0

    lax.fori_loop(0, tok // block, first_rows, 0)
    for j in range(CORES):
        step(j, sbuf)
        send_first(0, j)
    step(2, pbuf.at[0])
    step(3, pbuf.at[0])
    shared_expert()
    arrive(0, 1, 0, 0)
    next_tables(1)
    step(4, pbuf.at[1])
    step(5, pbuf.at[1])
    arrive(0, 1, 1, 0)
    next_tables(2)
    to_head_groups(0, w_query)
    step(6, pbuf.at[0])
    step(7, pbuf.at[0])
    arrive(0, 2, 0, 1)
    next_tables(3)
    for grp in range(GROUPS):
        for j in range(CORES):
            for q in range(seqs):
                ring_copy(0, 1, grp, j, q).wait_send()
    step(8, sbuf)
    step(9, sbuf)
    to_head_groups(1, w_key)
    arrive(0, 2, 1, 1)
    next_tables(4)
    for j in range(CORES):
        send_first(1, j)
    step(10, pbuf.at[1])
    step(11, pbuf.at[1])
    arrive(0, 3, 0, 0)
    to_head_groups(2, w_value)
    prefetch()
    combine(0, 0)
    arrive(0, 3, 1, 0)
    step(12, pbuf.at[0])
    combine(0, 1)
    step(13, pbuf.at[0])
    arrive(1, 1, 0, 1)
    begin_attention(0)
    attend(0, 4)
    arrive(1, 1, 1, 1)
    step(14, pbuf.at[1])
    step(15, pbuf.at[1])
    arrive(1, 2, 0, 0)
    attend(4, 8)
    end_attention(0)
    prefetch()
    arrive(1, 2, 1, 0)
    arrive(1, 3, 0, 1)
    combine(1, 0)
    arrive(1, 3, 1, 1)
    combine(1, 1)
    begin_attention(1)
    attend(0, 8)
    end_attention(1)
    out_copy(1).wait()

    for a, b in peers:
        key_copy(a, b).wait_send()
    for m, s in units:
        for j in range(CORES):
            table_copy(m, s, j).wait_send()
    for m in range(micros):
        for grp in range(GROUPS):
            for q in range(seqs):
                for s in range(1, chips):
                    for j in range(CORES):
                        if (m, s) != (0, 1):
                            ring_copy(m, s, grp, j, q).wait_send()
                rx_copy(m, grp, q).wait_send()
                if m == micros - 1:
                    y_copy(m, grp, q).wait_send()


def solution(mesh):
    stages = mesh.shape["pp"]
    ep_size = mesh.shape["ep"]
    tok_spec = P("pp", "data", "ep", None, None)
    vec_spec = P("pp", None)
    mat_spec = P("pp", None, None)
    head_spec = P("pp", None, None, None)

    def device_step(expert_out, expert_ids, slot_ids, gate_weights, residual, norm_moe, w_gate, w_up, w_down, norm_attn, w_query, w_key, w_value, w_out):
        micros, experts, slots_total, dim = expert_out.shape[1:]
        heads, head_dim = w_query.shape[2:]
        cap = slots_total // ep_size
        chips = ep_size // CORES
        half = dim // CORES
        seqs, seq_len, top_k = expert_ids.shape[2:]
        tok = seqs * seq_len
        group = tok // GROUPS
        width = 2 * head_dim
        head_groups = heads * head_dim // width

        def by_lane(x):
            return jnp.swapaxes(x[0], -1, -2)

        vmem = pl.BlockSpec(memory_space=pltpu.VMEM)
        anyspace = pl.BlockSpec(memory_space=pl.ANY)
        dma = pltpu.SemaphoreType.DMA
        out, _ = pl.pallas_call(
            functools.partial(boundary_kernel, stages, ep_size, seq_len),
            out_shape=[
                jax.ShapeDtypeStruct((micros, tok, dim), BF16),
                jax.ShapeDtypeStruct((3, head_groups, dim, width), BF16),
            ],
            in_specs=[anyspace, vmem, vmem, vmem, vmem, vmem, anyspace, anyspace, anyspace, vmem, anyspace, anyspace, anyspace, anyspace],
            out_specs=[anyspace, anyspace],
            scratch_shapes=[
                pltpu.VMEM((chips, CORES, experts, cap, half), BF16),
                pltpu.VMEM((2, CORES, experts, cap, half), BF16),
                pltpu.VMEM((2, 2, PARTS, tok, experts * cap), BF16),
                pltpu.VMEM((GROUPS, CORES, group, half), F32),
                pltpu.VMEM((2, GROUPS, CORES, group, half), F32),
                pltpu.VMEM((micros, chips - 1, GROUPS, CORES, group, half), F32),
                pltpu.VMEM((micros, GROUPS, group, half), F32),
                pltpu.VMEM((GROUPS, group, dim), BF16),
                pltpu.VMEM((micros, tok, dim), BF16),
                pltpu.VMEM((micros * tok, dim), BF16),
                pltpu.VMEM((2, 3, dim, width), BF16),
                pltpu.VMEM((2, width, dim), BF16),
                pltpu.VMEM((2, 256, heads, head_dim), BF16),
                pltpu.VMEM((2, head_groups, 256, width), BF16),
                pltpu.VMEM((tok, dim), BF16),
                pltpu.VMEM((tok, dim), F32),
                pltpu.VMEM((micros, GROUPS, 2, top_k, group), F32),
                pltpu.VMEM((micros, GROUPS, chips * CORES, 2, top_k, group), F32),
                pltpu.VMEM((micros, GROUPS, group, chips * CORES * 2 * top_k), F32),
                dma((micros, chips, CORES)), dma((micros, chips, CORES)), dma((2, CORES)),
                dma((micros, chips - 1, GROUPS, CORES, seqs // GROUPS)), dma((micros, chips - 1, GROUPS, CORES, seqs // GROUPS)),
                dma((micros, GROUPS, seqs // GROUPS)), dma((micros, GROUPS, seqs // GROUPS)),
                dma((micros, GROUPS, seqs // GROUPS)), dma((micros, GROUPS, seqs // GROUPS)),
                dma((chips, CORES)), dma((chips * CORES,)), dma((2, 4)), dma((2,)), dma((2,)), dma((micros,)),
                pltpu.SemaphoreType.REGULAR((chips,)),
            ],
            compiler_params=pltpu.CompilerParams(collective_id=0, has_side_effects=True, vmem_limit_bytes=67_000_000),
            cost_estimate=pl.CostEstimate(flops=50_000_000_000, bytes_accessed=200_000_000, transcendentals=0),
        )(expert_out[0], by_lane(expert_ids), by_lane(slot_ids), by_lane(gate_weights), residual[0].reshape(micros * tok, dim),
          norm_moe, w_gate[0], w_up[0], w_down[0], norm_attn, w_query[0], w_key[0], w_value[0], w_out[0].reshape(heads * head_dim, dim))
        return out.reshape(1, micros, seqs, seq_len, dim)

    in_specs = (tok_spec,) * 5 + (vec_spec, mat_spec, mat_spec, mat_spec, vec_spec, head_spec, head_spec, head_spec, head_spec)
    return jax.shard_map(device_step, mesh=mesh, in_specs=in_specs, out_specs=tok_spec, check_vma=False)
```

time: 544 us -> 205 us (0.38)
  waiting for transfers between devices: 327 us -> 0 us
  Pallas kernels: 0 us -> 200 us
  local copies, waits for them, and re-layouts: 92.7 us -> 3.16 us
  matrix products: 68.3 us -> 0 us
  other arithmetic: 32.2 us -> 0 us
  starting transfers between devices: 17 us -> 0 us
    all_to_all x2 -> x0, waiting for transfers between devices: 302 us -> none  [device_step(): received = lax.all_to_all(local_out, 'ep', 1, 0, tiled=True)]
    pallas_call x0 -> x1, Pallas kernels: none -> 200 us  [device_step(): pl.pallas_call(functools.partial(boundary_kernel, stages, ep_size, seq_le...]
    dot_general x12 -> x0, matrix products: 68.3 us -> none  [the longest x2 17.7 us: attention_block(): jnp.einsum('bqhe,bkhe->bhqk', queries, key_heads, preferred_element_type=...]
    gather x2 -> x0, local copies, waits for them, and re-layouts: 49.1 us -> none  [gather_combine(): picked = jnp.take(row_table, row_ids, axis=0, mode='clip')]
    reduce_sum x6 -> x0, other arithmetic: 29.4 us -> none  [the longest x2 24.5 us: gather_combine(): return jnp.sum(picked.astype(jnp.float32) * weights[..., None], axis=-2)]
    ppermute x2 -> x0, waiting for transfers between devices: 24.7 us -> none  [device_step(): incoming = lax.ppermute(combined, 'pp', shift_pairs)]
    another operation x2 -> x0, local copies, waits for them, and re-layouts: 21 us -> none  [device_step(): expert_out[0, micro_idx]]
    slice x1 -> x0, local copies, waits for them, and re-layouts: 18.6 us -> none  [device_step(): expert_out[0, micro_idx]]
  transfers between devices with their start and end apart: 4 -> 0, of which waited for: 3 -> 0; matrix products, arithmetic and copies ran while one was open for 20% -> 0% of each run, Pallas kernels for 0% -> 0%
where the time goes in v2:
time: 205 us; the launch traced here: 203 us
  Pallas kernels  200 us (98%)
  local copies, waits for them, and re-layouts  3.16 us (2%)
    pallas_call x1, Pallas kernels, device_step(): pl.pallas_call(functools.partial(boundary_kernel, stages, ep_size, seq_le...  200 us

profile of v2, /device:TPU:97, one launch (start us, length us, event | category | flops | bytes accessed | tf_op | source)
XLA Modules:
  0.0 202.9 jit_solution(9227389010119545499)
XLA Ops:
  0.0 199.7 %shard_map.136 = (bf16[2,256,2048]{2,1,0:T(8,128)(2,1)}, bf16[3,8,2048,256]{3,2,1,0:T(8,128)(2,1)}) custom-call(bf16[2,32,128,2048]{3,2,1,0:T(8,128)(2,1)} %bitcast.20, s32[2,4,8,64]{3,2,1,0:T(8,128)} %bitcast.29, s32[2,4,8,64]{3,2,1,0:T(8,128)} %bitcast.30, f32[2,4,8,64]{3,2,1,0:T(8,128)} %bitcast.31, bf16[512,2048]{1,0:T(8,128)(2,1)} %bitcast.25, ...), custom_call_target="tpu_custom_call" | custom-call | flops 49999998976 | bytes 200000000 | tf_op jit(solution)/shard_map/pallas_call | solution.py:517
  199.7 3.2 %copy.16 = bf16[1,2,4,64,2048]{4,3,2,1,0:T(8,128)(2,1)} copy(bf16[1,2,4,64,2048]{4,3,2,1,0:T(8,128)(2,1)} %bitcast.19) | data formatting | bytes 4194304

commit v3 on v2

--- a/solution.py
+++ b/solution.py
@@ -24,7 +24,7 @@
 def boundary_kernel(stages, ep_size, seq_len,
                     eo, ids, slots, gates, resid, norm_moe, w_gate, w_up, w_down, norm_attn, w_query, w_key, w_value, w_out,
                     out, w_heads,
-                    t_in, t_own, w, sbuf, pbuf, rbuf, rx, ysend, y_in, shared, pool_in, pool_out, raw, turned, xn, acc, kp, kr, kt,
+                    t_in, t_own, w, sbuf, pbuf, rbuf, rx, ysend, y_in, shared, pool_in, pool_out, raw, turned, xn, acc, qkv, mixed, kp, kr, kt,
                     tab_send, tab_recv, own_sem, ring_send, ring_recv, rx_send, rx_recv, y_send, y_recv,
                     key_send, key_recv, load_sem, raw_sem, turn_sem, out_sem, free_sem):
     micros, experts, slots_total, dim = eo.shape
@@ -51,14 +51,15 @@
     up = (pp + 1) % stages
     down = (pp + stages - 1) % stages
 
-    peers = [(a, b) for a in range(chips) for b in range(CORES) if (a, b) != (0, 0)]
-
-    def peer_id(a, b):
-        return ((chip + a) % chips) * CORES + (core + b) % CORES
+    peers = [(s, b) for s in range(1, chips + 1) for b in range(CORES) if (s, b) != (chips, 0)]
+
+    def peer_id(s, b):
+        there = (core + b) % CORES
+        return ((chip + s * (1 + there * (chips - 2))) % chips) * CORES + there
 
     barrier = pltpu.get_barrier_semaphore()
-    for a, b in peers:
-        pl.semaphore_signal(barrier, inc=1, device_id={"ep": peer_id(a, b)}, device_id_type=MESH)
+    for s, b in peers:
+        pl.semaphore_signal(barrier, inc=1, device_id={"ep": peer_id(s, b)}, device_id_type=MESH)
     pl.semaphore_signal(barrier, inc=1, device_id={"pp": down}, device_id_type=MESH)
 
     def dest_chip(s, stride):
@@ -104,46 +105,46 @@
     first = me * cap
     for m in range(micros):
         for grp in range(GROUPS):
-            key_rows, gate_rows = [], []
+            packed, gate_rows = [], []
             for q in range(seqs):
                 slot_here = slots[m, grp * seqs + q]
                 key_here = ids[m, grp * seqs + q] * cap + (slot_here - first)
-                key_rows.append(jnp.where(slot_here >= 0, key_here, -1).astype(F32))
+                packed.append(jnp.where(slot_here >= 0, key_here, -1).astype(F32))
                 gate_rows.append(gates[m, grp * seqs + q])
-            key_rows = jnp.concatenate(key_rows, axis=1)
+            packed = jnp.concatenate(packed, axis=1)
             gate_rows = jnp.concatenate(gate_rows, axis=1)
-            kp[m, grp, 0] = key_rows
+            kp[m, grp, 0] = packed
             kp[m, grp, 1] = gate_rows
-            kr[m, grp, (chips - 1) * CORES, 0] = key_rows
+            kr[m, grp, (chips - 1) * CORES, 0] = packed
             kr[m, grp, (chips - 1) * CORES, 1] = gate_rows
 
-    pl.semaphore_wait(barrier, len(peers) + 1)
-
-    def key_copy(a, b):
-        stride = 1 + ((core + b) % CORES) * (chips - 2)
-        place = ((chips - 1 + a * stride) % chips) * CORES + b
+    with jax.named_scope("barrier"):
+        pl.semaphore_wait(barrier, len(peers) + 1)
+
+    def key_copy(m, s, b):
+        place = (s - 1) * CORES + b
         return pltpu.make_async_remote_copy(
-            src_ref=kp, dst_ref=kr.at[:, :, place], send_sem=key_send.at[a, b], recv_sem=key_recv.at[place],
-            device_id={"ep": peer_id(a, b)}, device_id_type=MESH)
-
-    def key_arrival(place):
-        return pltpu.make_async_remote_copy(
-            src_ref=kp, dst_ref=kr.at[:, :, place], send_sem=key_send.at[0, 0], recv_sem=key_recv.at[place],
-            device_id={"ep": partner}, device_id_type=MESH)
-
-    for a, b in peers:
-        key_copy(a, b).start()
+            src_ref=kp.at[m], dst_ref=kr.at[m, :, place], send_sem=key_send.at[m, s - 1, b], recv_sem=key_recv.at[m, s - 1, b],
+            device_id={"ep": peer_id(s, b)}, device_id_type=MESH)
+
+    for m in range(micros):
+        for s, b in peers:
+            key_copy(m, s, b).start()
     for s in range(1, chips + 1):
         for j in range(CORES):
             table_copy(0, s, j).start()
     for copy in shared_loads():
         copy.start()
-    for place in range(chips * CORES):
-        if place != (chips - 1) * CORES:
-            key_arrival(place).wait_recv()
-    for m in range(micros):
+
+    key_rows = CORES * 2 * top_k
+
+    def take_keys(m, s):
+        for b in range(CORES):
+            if (s, b) in peers:
+                key_copy(m, s, b).wait_recv()
         for grp in range(GROUPS):
-            kt[m, grp] = kr[m, grp].reshape(chips * CORES * 2 * top_k, group).T
+            arrived = kr[m, grp, (s - 1) * CORES:s * CORES].reshape(key_rows, group)
+            kt[m, grp, :, (s - 1) * key_rows:s * key_rows] = arrived.T
 
     block = 32
     lane = lax.broadcasted_iota(jnp.int32, (block, rows), 1).astype(F32)
@@ -167,13 +168,17 @@
                 w[v % 2, h, part, pl.ds(r1, block), :] = value
 
     pieces = half // width
-
-    def step(v, target):
+    subs = len(units) * CORES
+
+    def step(v, target, groups, following):
         u, j = v // CORES, v % CORES
         m, s = units[u]
-        own_copy(u, j).wait()
-        table_copy(m, s, j).wait_recv()
-        span = tok // pieces
+        if groups[0] == 0:
+            own_copy(u, j).wait()
+            table_copy(m, s, j).wait_recv()
+        r0, count = groups[0] * group, len(groups) * group
+        builds = [(w_next, grp, b) for w_next, grp in following for b in range(group // block)]
+        per = -(-len(builds) // pieces)
 
         def body(n, _):
             c0 = pl.multiple_of(n * width, width)
@@ -181,22 +186,29 @@
             for h in range(2):
                 table = (t_own.at[u % 2, j] if h == 0 else t_in.at[s - 1, j])[:, :, pl.ds(c0, width)].reshape(rows, width)
                 for part in range(PARTS):
-                    term = dot(w[v % 2, h, part], table)
+                    term = dot(w[v % 2, h, part, r0:r0 + count], table)
                     total = term if total is None else total + term
-            for grp in range(GROUPS):
-                target[grp, j, :, pl.ds(c0, width)] = total[grp * group:(grp + 1) * group]
-            if v + 1 < len(units) * CORES:
-                for b in range(span // block):
-                    row = n * span + b * block
-                    build_rows(v + 1, row // group, pl.multiple_of(row % group, block))
+            for i, grp in enumerate(groups):
+                target[grp, j, :, pl.ds(c0, width)] = total[i * group:(i + 1) * group]
+            for b in range(per):
+                row = (n * per + b) * block
+                if len(following) == 1:
+                    build_rows(following[0][0], following[0][1], pl.multiple_of(row, block))
+                elif following:
+                    build_rows(following[0][0], row // group, pl.multiple_of(row % group, block))
             return 0
 
         lax.fori_loop(0, pieces, body, 0)
-        if j == CORES - 1:
+        if j == CORES - 1 and groups[-1] == GROUPS - 1:
             if u + 2 < len(units):
                 load_own(u + 2)
             if m == 0:
                 pl.semaphore_signal(free_sem.at[s - 1], inc=1, device_id={"ep": partner}, device_id_type=MESH)
+
+    def whole(v, target):
+        both = tuple(range(GROUPS))
+        with jax.named_scope("step"):
+            step(v, target, both, [(v + 1, grp) for grp in both] if v + 1 < subs else [])
 
     def next_tables(s):
         pl.semaphore_wait(free_sem.at[s - 1], 1)
@@ -211,8 +223,8 @@
             send_sem=ring_send.at[m, s - 1, grp, j, q], recv_sem=ring_recv.at[m, s - 1, grp, j, q],
             device_id={"ep": nxt}, device_id_type=MESH)
 
-    def send_first(m, j):
-        for grp in range(GROUPS):
+    def send_first(m, grp, order):
+        for j in order:
             for q in range(seqs):
                 ring_copy(m, 1, grp, j, q).start()
 
@@ -237,6 +249,8 @@
                     ring_copy(m, s + 1, grp, j, q).start()
                 elif j == 1:
                     rx_copy(m, grp, q).start()
+            if s == chips - 1:
+                combine(m, grp, q)
 
     def y_copy(m, grp, q):
         part = pl.ds(q * seq_len, seq_len)
@@ -245,22 +259,21 @@
             send_sem=y_send.at[m, grp, q], recv_sem=y_recv.at[m, grp, q],
             device_id={"pp": up}, device_id_type=MESH)
 
-    def combine(m, grp):
-        for q in range(seqs):
-            if m > 0:
-                y_copy(m - 1, grp, q).wait_send()
-            rx_copy(m, grp, q).wait_recv()
-
-            def body(b, _):
-                r0 = pl.multiple_of(q * seq_len + b * 16, 16)
-                r1 = pl.multiple_of(m * tok + grp * group + r0, 16)
-                for which, sums in ((core, rbuf.at[m, chips - 2, grp, 0]), (other, rx.at[m, grp])):
-                    base = resid[pl.ds(r1, 16), cols(which)].astype(F32) + shared[pl.ds(r1, 16), cols(which)].astype(F32)
-                    ysend[grp, pl.ds(r0, 16), cols(which)] = (base + sums[pl.ds(r0, 16), :]).astype(BF16)
-                return 0
-
-            lax.fori_loop(0, seq_len // 16, body, 0)
-            y_copy(m, grp, q).start()
+    def combine(m, grp, q):
+        if m > 0:
+            y_copy(m - 1, grp, q).wait_send()
+        rx_copy(m, grp, q).wait_recv()
+
+        def body(b, _):
+            r0 = pl.multiple_of(q * seq_len + b * 16, 16)
+            r1 = pl.multiple_of(m * tok + grp * group + r0, 16)
+            for which, sums in ((core, rbuf.at[m, chips - 2, grp, 0]), (other, rx.at[m, grp])):
+                base = resid[pl.ds(r1, 16), cols(which)].astype(F32) + shared[pl.ds(r1, 16), cols(which)].astype(F32)
+                ysend[grp, pl.ds(r0, 16), cols(which)] = (base + sums[pl.ds(r0, 16), :]).astype(BF16)
+            return 0
+
+        lax.fori_loop(0, seq_len // 16, body, 0)
+        y_copy(m, grp, q).start()
 
     def normalize(source, base, count, gain):
         def body(b, _):
@@ -293,93 +306,105 @@
 
         lax.fori_loop(0, micros, body, 0)
 
-    chunk = raw.shape[1]
+    depth, chunk = raw.shape[:2]
 
     def to_head_groups(kind, source):
         count = dim // chunk
 
         def fetch(c):
-            return pltpu.make_async_copy(source.at[pl.ds(pl.multiple_of(c * chunk, chunk), chunk)], raw.at[c % 2], raw_sem.at[c % 2])
+            return pltpu.make_async_copy(source.at[pl.ds(pl.multiple_of(c * chunk, chunk), chunk)], raw.at[c % depth], raw_sem.at[c % depth])
 
         def flush(c):
-            return pltpu.make_async_copy(turned.at[c % 2], w_heads.at[kind, :, pl.ds(pl.multiple_of(c * chunk, chunk), chunk)], turn_sem.at[c % 2])
-
-        fetch(0).start()
+            return pltpu.make_async_copy(turned.at[c % depth], w_heads.at[kind, :, pl.ds(pl.multiple_of(c * chunk, chunk), chunk)], turn_sem.at[c % depth])
+
+        for c in range(depth - 1):
+            fetch(c).start()
 
         def body(c, _):
-            @pl.when(c + 1 < count)
+            @pl.when(c + depth - 1 < count)
             def _():
-                fetch(c + 1).start()
+                fetch(c + depth - 1).start()
             fetch(c).wait()
 
-            @pl.when(c >= 2)
+            @pl.when(c >= depth)
             def _():
-                flush(c - 2).wait()
+                flush(c - depth).wait()
 
             def turn(b, _):
                 r0 = pl.multiple_of(b * 32, 32)
-                value = jnp.swapaxes(raw[c % 2, pl.ds(r0, 32)], 0, 1)
+                value = jnp.swapaxes(raw[c % depth, pl.ds(r0, 32)], 0, 1)
                 for h in range(heads):
                     place = (h * head_dim) % width
-                    turned[c % 2, h * head_dim // width, pl.ds(r0, 32), place:place + head_dim] = value[h]
+                    turned[c % depth, h * head_dim // width, pl.ds(r0, 32), place:place + head_dim] = value[h]
                 return 0
 
             lax.fori_loop(0, chunk // 32, turn, 0)
             flush(c).start()
             return 0
 
-        lax.fori_loop(0, count, body, 0)
-        flush(count - 2).wait()
-        flush(count - 1).wait()
-
-    def weight_loads(g, slot):
-        loads = [pltpu.make_async_copy(w_heads.at[kind, g], pool_in.at[slot, kind], load_sem.at[slot, kind]) for kind in range(3)]
-        loads.append(pltpu.make_async_copy(w_out.at[pl.ds(pl.multiple_of(g * width, width), width)], pool_out.at[slot], load_sem.at[slot, 3]))
-        return loads
+        with jax.named_scope("rewrite"):
+            lax.fori_loop(0, count, body, 0)
+            for c in range(count - depth, count):
+                flush(c).wait()
+
+    def in_loads(g, slot):
+        return [pltpu.make_async_copy(w_heads.at[kind, g], pool_in.at[slot, kind], load_sem.at[slot, kind]) for kind in range(3)]
+
+    def out_load(g, slot):
+        return pltpu.make_async_copy(w_out.at[pl.ds(pl.multiple_of(g * width, width), width)], pool_out.at[slot], load_sem.at[slot, 3])
 
     def prefetch():
         for g in range(2):
-            for copy in weight_loads(g, g):
+            for copy in in_loads(g, g):
                 copy.start()
+            out_load(g, g).start()
 
     span_q = 128
     score_scale = 1.0 / math.sqrt(head_dim)
 
-    def attend(g0, g1):
+    def project(g, slot):
+        for kind in range(3):
+            qkv[slot, kind] = dot(xn[...], pool_in[slot, kind]).astype(BF16)
+
+    def mix(slot):
         row = lax.broadcasted_iota(jnp.int32, (span_q, span_q), 0)
         col = lax.broadcasted_iota(jnp.int32, (span_q, span_q), 1)
         visible = (row >= col) & (row // seq_len == col // seq_len)
-
+        for r in range(tok // span_q):
+            line = []
+            for h in range(width // head_dim):
+                part = (slice(r * span_q, (r + 1) * span_q), slice(h * head_dim, (h + 1) * head_dim))
+                scores = lax.dot_general(qkv[(slot, 0) + part], qkv[(slot, 1) + part], (((1,), (1,)), ((), ())), preferred_element_type=F32) * score_scale
+                scores = jnp.where(visible, scores, -1e30)
+                probs = jnp.exp(scores - jnp.max(scores, axis=-1, keepdims=True))
+                total = jnp.sum(probs, axis=-1, keepdims=True)
+                line.append((dot(probs.astype(BF16), qkv[(slot, 2) + part]) / total).astype(BF16))
+            mixed[slot, r * span_q:(r + 1) * span_q, :] = jnp.concatenate(line, axis=1)
+        for n in range(dim // (2 * width)):
+            span = pl.ds(n * 2 * width, 2 * width)
+            acc[:, span] += dot(mixed[slot], pool_out[slot, :, span])
+
+    def attend(g0, g1):
         def body(g, _):
             slot = g % 2
-            for copy in weight_loads(g, slot):
+            for copy in in_loads(g, slot):
                 copy.wait()
-            queries = dot(xn[...], pool_in[slot, 0]).astype(BF16)
-            key_heads = dot(xn[...], pool_in[slot, 1]).astype(BF16)
-            value_heads = dot(xn[...], pool_in[slot, 2]).astype(BF16)
-            mixed = []
-            for r in range(tok // span_q):
-                line = []
-                for h in range(width // head_dim):
-                    part = (slice(r * span_q, (r + 1) * span_q), slice(h * head_dim, (h + 1) * head_dim))
-                    scores = lax.dot_general(queries[part], key_heads[part], (((1,), (1,)), ((), ())), preferred_element_type=F32) * score_scale
-                    scores = jnp.where(visible, scores, -1e30)
-                    probs = jnp.exp(scores - jnp.max(scores, axis=-1, keepdims=True))
-                    total = jnp.sum(probs, axis=-1, keepdims=True)
-                    line.append((dot(probs.astype(BF16), value_heads[part]) / total).astype(BF16))
-                mixed.append(jnp.concatenate(line, axis=1))
-            mixed = jnp.concatenate(mixed, axis=0)
-            for n in range(dim // (2 * width)):
-                span = pl.ds(n * 2 * width, 2 * width)
-                acc[:, span] += dot(mixed, pool_out[slot, :, span])
+            out_load(g - 1, 1 - slot).wait()
+            mix(1 - slot)
+            project(g, slot)
 
             @pl.when(g + 2 < head_groups)
             def _():
-                for copy in weight_loads(g + 2, slot):
+                for copy in in_loads(g + 2, slot):
                     copy.start()
-            return 0
-
-        lax.fori_loop(g0, g1, body, 0)
+
+            @pl.when(g + 1 < head_groups)
+            def _():
+                out_load(g + 1, 1 - slot).start()
+            return 0
+
+        with jax.named_scope("attend"):
+            lax.fori_loop(g0, g1, body, 0)
 
     def out_copy(m):
         return pltpu.make_async_copy(xn, out.at[m], out_sem.at[m])
@@ -397,8 +422,16 @@
             return 0
 
         lax.fori_loop(0, tok // 16, clear, 0)
+        for copy in in_loads(0, 0):
+            copy.wait()
+        project(0, 0)
+        for copy in in_loads(2, 0):
+            copy.start()
 
     def end_attention(m):
+        out_load(head_groups - 1, 1).wait()
+        mix(1)
+
         def body(b, _):
             r0 = pl.multiple_of(b * 16, 16)
             proj = acc[pl.ds(r0, 16), :].astype(BF16).astype(F32)
@@ -407,72 +440,82 @@
         lax.fori_loop(0, tok // 16, body, 0)
         out_copy(m).start()
 
+    def scoped(name, task, *args):
+        with jax.named_scope(name):
+            task(*args)
+
     def first_rows(b, _):
-        row = b * block
-        build_rows(0, row // group, pl.multiple_of(row % group, block))
+        build_rows(0, 0, pl.multiple_of(b * block, block))
         return 0
 
-    lax.fori_loop(0, tok // block, first_rows, 0)
-    for j in range(CORES):
-        step(j, sbuf)
-        send_first(0, j)
-    step(2, pbuf.at[0])
-    step(3, pbuf.at[0])
-    shared_expert()
-    arrive(0, 1, 0, 0)
+    scoped("keys", take_keys, 0, 1)
+    scoped("build", lax.fori_loop, 0, group // block, first_rows, 0)
+    for grp in range(GROUPS):
+        for j in range(CORES):
+            if (grp, j) == (1, 1):
+                following = [(2, 0), (2, 1)]
+            else:
+                following = [((j + 1) % CORES, grp + j)]
+            scoped("half", step, j, sbuf, (grp,), following)
+            send_first(0, grp, (j,))
+            if (grp, j) == (0, 1):
+                for m, s in units[1:]:
+                    scoped("keys", take_keys, m, s)
+    whole(2, pbuf.at[0])
+    whole(3, pbuf.at[0])
+    scoped("shared", shared_expert)
+    scoped("arrive", arrive, 0, 1, 0, 0)
     next_tables(1)
-    step(4, pbuf.at[1])
-    step(5, pbuf.at[1])
-    arrive(0, 1, 1, 0)
+    to_head_groups(0, w_query)
+    whole(4, pbuf.at[1])
+    whole(5, pbuf.at[1])
+    scoped("arrive", arrive, 0, 1, 1, 0)
     next_tables(2)
-    to_head_groups(0, w_query)
-    step(6, pbuf.at[0])
-    step(7, pbuf.at[0])
-    arrive(0, 2, 0, 1)
+    whole(6, pbuf.at[0])
+    whole(7, pbuf.at[0])
+    to_head_groups(1, w_key)
+    scoped("arrive", arrive, 0, 2, 0, 1)
     next_tables(3)
     for grp in range(GROUPS):
         for j in range(CORES):
             for q in range(seqs):
                 ring_copy(0, 1, grp, j, q).wait_send()
-    step(8, sbuf)
-    step(9, sbuf)
-    to_head_groups(1, w_key)
-    arrive(0, 2, 1, 1)
-    next_tables(4)
-    for j in range(CORES):
-        send_first(1, j)
-    step(10, pbuf.at[1])
-    step(11, pbuf.at[1])
-    arrive(0, 3, 0, 0)
+    whole(8, sbuf)
+    whole(9, sbuf)
     to_head_groups(2, w_value)
     prefetch()
-    combine(0, 0)
-    arrive(0, 3, 1, 0)
-    step(12, pbuf.at[0])
-    combine(0, 1)
-    step(13, pbuf.at[0])
-    arrive(1, 1, 0, 1)
-    begin_attention(0)
-    attend(0, 4)
-    arrive(1, 1, 1, 1)
-    step(14, pbuf.at[1])
-    step(15, pbuf.at[1])
-    arrive(1, 2, 0, 0)
-    attend(4, 8)
-    end_attention(0)
+    scoped("arrive", arrive, 0, 2, 1, 1)
+    next_tables(4)
+    for grp in range(GROUPS):
+        send_first(1, grp, (1, 0))
+    whole(10, pbuf.at[1])
+    whole(11, pbuf.at[1])
+    scoped("final", arrive, 0, 3, 0, 0)
+    scoped("final", arrive, 0, 3, 1, 0)
+    whole(12, pbuf.at[0])
+    whole(13, pbuf.at[0])
+    scoped("arrive", arrive, 1, 1, 0, 1)
+    scoped("begin", begin_attention, 0)
+    attend(1, 3)
+    scoped("arrive", arrive, 1, 1, 1, 1)
+    whole(14, pbuf.at[1])
+    whole(15, pbuf.at[1])
+    attend(3, 5)
+    scoped("arrive", arrive, 1, 2, 0, 0)
+    attend(5, 8)
+    scoped("end", end_attention, 0)
     prefetch()
-    arrive(1, 2, 1, 0)
-    arrive(1, 3, 0, 1)
-    combine(1, 0)
-    arrive(1, 3, 1, 1)
-    combine(1, 1)
-    begin_attention(1)
-    attend(0, 8)
-    end_attention(1)
-    out_copy(1).wait()
-
-    for a, b in peers:
-        key_copy(a, b).wait_send()
+    scoped("arrive", arrive, 1, 2, 1, 0)
+    scoped("final", arrive, 1, 3, 0, 1)
+    scoped("final", arrive, 1, 3, 1, 1)
+    scoped("begin", begin_attention, 1)
+    attend(1, 8)
+    scoped("end", end_attention, 1)
+    scoped("out", out_copy(1).wait)
+
+    for m in range(micros):
+        for s, b in peers:
+            key_copy(m, s, b).wait_send()
     for m, s in units:
         for j in range(CORES):
             table_copy(m, s, j).wait_send()
@@ -535,10 +578,12 @@
                 pltpu.VMEM((micros * tok, dim), BF16),
                 pltpu.VMEM((2, 3, dim, width), BF16),
                 pltpu.VMEM((2, width, dim), BF16),
-                pltpu.VMEM((2, 256, heads, head_dim), BF16),
-                pltpu.VMEM((2, head_groups, 256, width), BF16),
+                pltpu.VMEM((4, 128, heads, head_dim), BF16),
+                pltpu.VMEM((4, head_groups, 128, width), BF16),
                 pltpu.VMEM((tok, dim), BF16),
                 pltpu.VMEM((tok, dim), F32),
+                pltpu.VMEM((2, 3, tok, width), BF16),
+                pltpu.VMEM((2, tok, width), BF16),
                 pltpu.VMEM((micros, GROUPS, 2, top_k, group), F32),
                 pltpu.VMEM((micros, GROUPS, chips * CORES, 2, top_k, group), F32),
                 pltpu.VMEM((micros, GROUPS, group, chips * CORES * 2 * top_k), F32),
@@ -546,7 +591,7 @@
                 dma((micros, chips - 1, GROUPS, CORES, seqs // GROUPS)), dma((micros, chips - 1, GROUPS, CORES, seqs // GROUPS)),
                 dma((micros, GROUPS, seqs // GROUPS)), dma((micros, GROUPS, seqs // GROUPS)),
                 dma((micros, GROUPS, seqs // GROUPS)), dma((micros, GROUPS, seqs // GROUPS)),
-                dma((chips, CORES)), dma((chips * CORES,)), dma((2, 4)), dma((2,)), dma((2,)), dma((micros,)),
+                dma((micros, chips, CORES)), dma((micros, chips, CORES)), dma((2, 4)), dma((4,)), dma((4,)), dma((micros,)),
                 pltpu.SemaphoreType.REGULAR((chips,)),
             ],
             compiler_params=pltpu.CompilerParams(collective_id=0, has_side_effects=True, vmem_limit_bytes=67_000_000),

time: 205 us -> 192 us (0.937)
  Pallas kernels: 200 us -> 188 us
    pallas_call x1, Pallas kernels: 200 us -> 188 us  [device_step(): pl.pallas_call(functools.partial(boundary_kernel, stages, ep_size, seq_le...]
where the time goes in v3:
time: 192 us; the launch traced here: 191 us
  Pallas kernels  188 us (98%)
  local copies, waits for them, and re-layouts  3.16 us (2%)
    pallas_call x1, Pallas kernels, device_step(): pl.pallas_call(functools.partial(boundary_kernel, stages, ep_size, seq_le...  188 us

profile of v3, /device:TPU:97, one launch (start us, length us, event | category | flops | bytes accessed | tf_op | source)
XLA Modules:
  0.0 191.1 jit_solution(18342360337856419084)
XLA Ops:
  0.0 187.9 %shard_map.136 = (bf16[2,256,2048]{2,1,0:T(8,128)(2,1)}, bf16[3,8,2048,256]{3,2,1,0:T(8,128)(2,1)}) custom-call(bf16[2,32,128,2048]{3,2,1,0:T(8,128)(2,1)} %bitcast.20, s32[2,4,8,64]{3,2,1,0:T(8,128)} %bitcast.29, s32[2,4,8,64]{3,2,1,0:T(8,128)} %bitcast.30, f32[2,4,8,64]{3,2,1,0:T(8,128)} %bitcast.31, bf16[512,2048]{1,0:T(8,128)(2,1)} %bitcast.25, ...), custom_call_target="tpu_custom_call" | custom-call | flops 49999998976 | bytes 200000000 | tf_op jit(solution)/shard_map/pallas_call | solution.py:560
  187.9 3.2 %copy.16 = bf16[1,2,4,64,2048]{4,3,2,1,0:T(8,128)(2,1)} copy(bf16[1,2,4,64,2048]{4,3,2,1,0:T(8,128)(2,1)} %bitcast.19) | data formatting | bytes 4194304

commit v4 on v3

--- a/solution.py
+++ b/solution.py
@@ -22,11 +22,11 @@
 
 
 def boundary_kernel(stages, ep_size, seq_len,
-                    eo, ids, slots, gates, resid, norm_moe, w_gate, w_up, w_down, norm_attn, w_query, w_key, w_value, w_out,
+                    eo, ids, slots, gates, resid_hbm, norm_moe, w_gate, w_up, w_down, norm_attn, w_query, w_key, w_value, w_out,
                     out, w_heads,
-                    t_in, t_own, w, sbuf, pbuf, rbuf, rx, ysend, y_in, shared, pool_in, pool_out, raw, turned, xn, acc, qkv, mixed, kp, kr, kt,
+                    t_in, t_own, w, sbuf, pbuf, rbuf, rx, ysend, y_in, resid, shared, pool_in, pool_out, raw, turned, xn, acc, qkv, mixed, kp, kr, kt,
                     tab_send, tab_recv, own_sem, ring_send, ring_recv, rx_send, rx_recv, y_send, y_recv,
-                    key_send, key_recv, load_sem, raw_sem, turn_sem, out_sem, free_sem):
+                    key_send, key_recv, load_sem, raw_sem, turn_sem, out_sem, resid_sem, free_sem):
     micros, experts, slots_total, dim = eo.shape
     chips = ep_size // CORES
     cap = slots_total // ep_size
@@ -90,6 +90,8 @@
 
     load_own(0)
     load_own(1)
+    resid_copy = pltpu.make_async_copy(resid_hbm, resid, resid_sem.at[0])
+    resid_copy.start()
 
     def shared_loads():
         halves = [pl.ds(0, width), pl.ds(width, width)]
@@ -240,8 +242,8 @@
             send_sem=rx_send.at[m, grp, q], recv_sem=rx_recv.at[m, grp, q],
             device_id={"ep": partner}, device_id_type=MESH)
 
-    def arrive(m, s, grp, slot):
-        for q in range(seqs):
+    def arrive(m, s, grp, slot, which=None):
+        for q in range(seqs) if which is None else which:
             for j in (1, 0):
                 ring_copy(m, s, grp, j, q).wait_recv()
                 add_in(m, s, grp, j, q, slot)
@@ -275,23 +277,24 @@
         lax.fori_loop(0, seq_len // 16, body, 0)
         y_copy(m, grp, q).start()
 
-    def normalize(source, base, count, gain):
+    def normalize(source, base, place, count, gain):
         def body(b, _):
-            r0 = pl.multiple_of(b * 16, 16)
+            r0 = b * 16
             values = source[pl.ds(pl.multiple_of(base + r0, 16), 16), :].astype(F32)
             inv_rms = lax.rsqrt(jnp.mean(values * values, axis=-1, keepdims=True) + EPSILON)
-            xn[pl.ds(r0, 16), :] = (values * inv_rms * gain[...]).astype(BF16)
-            return 0
-        lax.fori_loop(0, count // 16, body, 0)
+            xn[pl.ds(pl.multiple_of(place + r0, 16), 16), :] = (values * inv_rms * gain[...]).astype(BF16)
+            return 0
+        lax.fori_loop(0, count // 16, body, 0, unroll=2)
 
     def shared_expert():
         for copy in shared_loads():
             copy.wait()
+        resid_copy.wait()
         gate_refs = (pool_in.at[0, 0], pool_in.at[0, 1])
         up_refs = (pool_in.at[0, 2], pool_in.at[1, 0])
 
         def body(m, _):
-            normalize(resid, m * tok, tok, norm_moe)
+            normalize(resid, m * tok, 0, tok, norm_moe)
             hidden = []
             for f in range(ff // width):
                 gate_act = dot(xn[...], gate_refs[f][...])
@@ -353,8 +356,10 @@
     def out_load(g, slot):
         return pltpu.make_async_copy(w_out.at[pl.ds(pl.multiple_of(g * width, width), width)], pool_out.at[slot], load_sem.at[slot, 3])
 
+    ways = pool_out.shape[0]
+
     def prefetch():
-        for g in range(2):
+        for g in range(ways):
             for copy in in_loads(g, g):
                 copy.start()
             out_load(g, g).start()
@@ -362,81 +367,99 @@
     span_q = 128
     score_scale = 1.0 / math.sqrt(head_dim)
 
-    def project(g, slot):
-        for kind in range(3):
-            qkv[slot, kind] = dot(xn[...], pool_in[slot, kind]).astype(BF16)
-
-    def mix(slot):
+    spans = [(slice(r * span_q, (r + 1) * span_q), slice(h * head_dim, (h + 1) * head_dim))
+             for r in range(tok // span_q) for h in range(width // head_dim)]
+
+    def project(g, slot, kind):
+        qkv[slot, kind] = dot(xn[...], pool_in[g % ways, kind]).astype(BF16)
+
+    def score(slot):
         row = lax.broadcasted_iota(jnp.int32, (span_q, span_q), 0)
         col = lax.broadcasted_iota(jnp.int32, (span_q, span_q), 1)
         visible = (row >= col) & (row // seq_len == col // seq_len)
-        for r in range(tok // span_q):
-            line = []
-            for h in range(width // head_dim):
-                part = (slice(r * span_q, (r + 1) * span_q), slice(h * head_dim, (h + 1) * head_dim))
-                scores = lax.dot_general(qkv[(slot, 0) + part], qkv[(slot, 1) + part], (((1,), (1,)), ((), ())), preferred_element_type=F32) * score_scale
-                scores = jnp.where(visible, scores, -1e30)
-                probs = jnp.exp(scores - jnp.max(scores, axis=-1, keepdims=True))
-                total = jnp.sum(probs, axis=-1, keepdims=True)
-                line.append((dot(probs.astype(BF16), qkv[(slot, 2) + part]) / total).astype(BF16))
-            mixed[slot, r * span_q:(r + 1) * span_q, :] = jnp.concatenate(line, axis=1)
+        scores = []
+        for span in spans:
+            product = lax.dot_general(qkv[(slot, 0) + span], qkv[(slot, 1) + span], (((1,), (1,)), ((), ())), preferred_element_type=F32)
+            scores.append(jnp.where(visible, product * score_scale, -1e30))
+        return scores
+
+    def weigh(slot, scores):
+        weighed = []
+        for values in scores:
+            probs = jnp.exp(values - jnp.max(values, axis=-1, keepdims=True))
+            weighed.append((probs.astype(BF16), jnp.sum(probs, axis=-1, keepdims=True)))
+        for span, (probs, total) in zip(spans, weighed):
+            mixed[(slot,) + span] = (dot(probs, qkv[(slot, 2) + span]) / total).astype(BF16)
+
+    def project_out(g, slot):
         for n in range(dim // (2 * width)):
             span = pl.ds(n * 2 * width, 2 * width)
-            acc[:, span] += dot(mixed[slot], pool_out[slot, :, span])
-
-    def attend(g0, g1):
-        def body(g, _):
-            slot = g % 2
-            for copy in in_loads(g, slot):
-                copy.wait()
-            out_load(g - 1, 1 - slot).wait()
-            mix(1 - slot)
-            project(g, slot)
-
-            @pl.when(g + 2 < head_groups)
-            def _():
-                for copy in in_loads(g + 2, slot):
-                    copy.start()
-
-            @pl.when(g + 1 < head_groups)
-            def _():
-                out_load(g + 1, 1 - slot).start()
+            acc[:, span] += dot(mixed[slot], pool_out[g % ways, :, span])
+
+    def advance(g, slot):
+        for copy in in_loads(g, g % ways):
+            copy.wait()
+        out_load(g - 1, (g - 1) % ways).wait()
+        project(g, slot, 0)
+        scores = score(1 - slot)
+        project(g, slot, 1)
+        weigh(1 - slot, scores)
+        project(g, slot, 2)
+        project_out(g - 1, 1 - slot)
+
+        @pl.when(g + ways < head_groups)
+        def _():
+            for copy in in_loads(g + ways, g % ways):
+                copy.start()
+
+        @pl.when(g - 1 + ways < head_groups)
+        def _():
+            out_load(g - 1 + ways, (g - 1) % ways).start()
+
+    def attend(g0, pairs):
+        def body(i, _):
+            advance(g0 + 2 * i, g0 % 2)
+            advance(g0 + 2 * i + 1, 1 - g0 % 2)
             return 0
 
         with jax.named_scope("attend"):
-            lax.fori_loop(g0, g1, body, 0)
+            lax.fori_loop(0, pairs, body, 0)
 
     def out_copy(m):
         return pltpu.make_async_copy(xn, out.at[m], out_sem.at[m])
 
-    def begin_attention(m):
-        for grp in range(GROUPS):
-            for q in range(seqs):
-                y_copy(m, grp, q).wait_recv()
-        if m > 0:
-            out_copy(m - 1).wait()
-        normalize(y_in.at[m], 0, tok, norm_attn)
-
+    def take_y(m, grp, q):
+        y_copy(m, grp, q).wait_recv()
+        start = grp * group + q * seq_len
+        normalize(y_in.at[m], start, start, seq_len, norm_attn)
+
+    def clear_sums():
         def clear(b, _):
             acc[pl.ds(pl.multiple_of(b * 16, 16), 16), :] = jnp.zeros((16, dim), F32)
             return 0
 
         lax.fori_loop(0, tok // 16, clear, 0)
+
+    def begin_attention():
         for copy in in_loads(0, 0):
             copy.wait()
-        project(0, 0)
-        for copy in in_loads(2, 0):
+        for kind in range(3):
+            project(0, 0, kind)
+        for copy in in_loads(ways, 0):
             copy.start()
 
     def end_attention(m):
-        out_load(head_groups - 1, 1).wait()
-        mix(1)
+        advance(head_groups - 1, 1)
+        out_load(head_groups - 1, (head_groups - 1) % ways).wait()
+        weigh(1, score(1))
+        project_out(head_groups - 1, 1)
 
         def body(b, _):
             r0 = pl.multiple_of(b * 16, 16)
             proj = acc[pl.ds(r0, 16), :].astype(BF16).astype(F32)
             xn[pl.ds(r0, 16), :] = (y_in[m, pl.ds(r0, 16), :].astype(F32) + proj).astype(BF16)
             return 0
+
         lax.fori_loop(0, tok // 16, body, 0)
         out_copy(m).start()
 
@@ -473,7 +496,6 @@
     next_tables(2)
     whole(6, pbuf.at[0])
     whole(7, pbuf.at[0])
-    to_head_groups(1, w_key)
     scoped("arrive", arrive, 0, 2, 0, 1)
     next_tables(3)
     for grp in range(GROUPS):
@@ -482,8 +504,7 @@
                 ring_copy(0, 1, grp, j, q).wait_send()
     whole(8, sbuf)
     whole(9, sbuf)
-    to_head_groups(2, w_value)
-    prefetch()
+    to_head_groups(1, w_key)
     scoped("arrive", arrive, 0, 2, 1, 1)
     next_tables(4)
     for grp in range(GROUPS):
@@ -491,25 +512,36 @@
     whole(10, pbuf.at[1])
     whole(11, pbuf.at[1])
     scoped("final", arrive, 0, 3, 0, 0)
+    to_head_groups(2, w_value)
+    prefetch()
     scoped("final", arrive, 0, 3, 1, 0)
     whole(12, pbuf.at[0])
     whole(13, pbuf.at[0])
     scoped("arrive", arrive, 1, 1, 0, 1)
-    scoped("begin", begin_attention, 0)
+    clear_sums()
+    for grp in range(GROUPS):
+        for q in range(seqs):
+            scoped("take_y", take_y, 0, grp, q)
+    scoped("begin", begin_attention)
     attend(1, 3)
     scoped("arrive", arrive, 1, 1, 1, 1)
     whole(14, pbuf.at[1])
     whole(15, pbuf.at[1])
-    attend(3, 5)
-    scoped("arrive", arrive, 1, 2, 0, 0)
-    attend(5, 8)
     scoped("end", end_attention, 0)
     prefetch()
+    scoped("arrive", arrive, 1, 2, 0, 0)
     scoped("arrive", arrive, 1, 2, 1, 0)
+    out_copy(0).wait()
+    clear_sums()
     scoped("final", arrive, 1, 3, 0, 1)
-    scoped("final", arrive, 1, 3, 1, 1)
-    scoped("begin", begin_attention, 1)
-    attend(1, 8)
+    scoped("take_y", take_y, 1, 0, 0)
+    scoped("final", arrive, 1, 3, 1, 1, (0,))
+    scoped("take_y", take_y, 1, 0, 1)
+    scoped("final", arrive, 1, 3, 1, 1, (1,))
+    scoped("take_y", take_y, 1, 1, 0)
+    scoped("take_y", take_y, 1, 1, 1)
+    scoped("begin", begin_attention)
+    attend(1, 3)
     scoped("end", end_attention, 1)
     scoped("out", out_copy(1).wait)
 
@@ -563,7 +595,7 @@
                 jax.ShapeDtypeStruct((micros, tok, dim), BF16),
                 jax.ShapeDtypeStruct((3, head_groups, dim, width), BF16),
             ],
-            in_specs=[anyspace, vmem, vmem, vmem, vmem, vmem, anyspace, anyspace, anyspace, vmem, anyspace, anyspace, anyspace, anyspace],
+            in_specs=[anyspace, vmem, vmem, vmem, anyspace, vmem, anyspace, anyspace, anyspace, vmem, anyspace, anyspace, anyspace, anyspace],
             out_specs=[anyspace, anyspace],
             scratch_shapes=[
                 pltpu.VMEM((chips, CORES, experts, cap, half), BF16),
@@ -576,10 +608,11 @@
                 pltpu.VMEM((GROUPS, group, dim), BF16),
                 pltpu.VMEM((micros, tok, dim), BF16),
                 pltpu.VMEM((micros * tok, dim), BF16),
-                pltpu.VMEM((2, 3, dim, width), BF16),
-                pltpu.VMEM((2, width, dim), BF16),
-                pltpu.VMEM((4, 128, heads, head_dim), BF16),
-                pltpu.VMEM((4, head_groups, 128, width), BF16),
+                pltpu.VMEM((micros * tok, dim), BF16),
+                pltpu.VMEM((3, 3, dim, width), BF16),
+                pltpu.VMEM((3, width, dim), BF16),
+                pltpu.VMEM((3, 128, heads, head_dim), BF16),
+                pltpu.VMEM((3, head_groups, 128, width), BF16),
                 pltpu.VMEM((tok, dim), BF16),
                 pltpu.VMEM((tok, dim), F32),
                 pltpu.VMEM((2, 3, tok, width), BF16),
@@ -591,7 +624,7 @@
                 dma((micros, chips - 1, GROUPS, CORES, seqs // GROUPS)), dma((micros, chips - 1, GROUPS, CORES, seqs // GROUPS)),
                 dma((micros, GROUPS, seqs // GROUPS)), dma((micros, GROUPS, seqs // GROUPS)),
                 dma((micros, GROUPS, seqs // GROUPS)), dma((micros, GROUPS, seqs // GROUPS)),
-                dma((micros, chips, CORES)), dma((micros, chips, CORES)), dma((2, 4)), dma((4,)), dma((4,)), dma((micros,)),
+                dma((micros, chips, CORES)), dma((micros, chips, CORES)), dma((3, 4)), dma((3,)), dma((3,)), dma((micros,)), dma((1,)),
                 pltpu.SemaphoreType.REGULAR((chips,)),
             ],
             compiler_params=pltpu.CompilerParams(collective_id=0, has_side_effects=True, vmem_limit_bytes=67_000_000),

time: 192 us -> 178 us (0.927)
  Pallas kernels: 188 us -> 173 us
    pallas_call x1, Pallas kernels: 188 us -> 173 us  [device_step(): pl.pallas_call(functools.partial(boundary_kernel, stages, ep_size, seq_le...]
where the time goes in v4:
time: 178 us; the launch traced here: 177 us
  Pallas kernels  173 us (97%)
  local copies, waits for them, and re-layouts  3.16 us (2%)
    pallas_call x1, Pallas kernels, device_step(): pl.pallas_call(functools.partial(boundary_kernel, stages, ep_size, seq_le...  173 us

profile of v4, /device:TPU:97, one launch (start us, length us, event | category | flops | bytes accessed | tf_op | source)
XLA Modules:
  0.0 176.6 jit_solution(3316173880686631235)
XLA Ops:
  0.0 173.4 %shard_map.136 = (bf16[2,256,2048]{2,1,0:T(8,128)(2,1)}, bf16[3,8,2048,256]{3,2,1,0:T(8,128)(2,1)}) custom-call(bf16[2,32,128,2048]{3,2,1,0:T(8,128)(2,1)} %bitcast.20, s32[2,4,8,64]{3,2,1,0:T(8,128)} %bitcast.29, s32[2,4,8,64]{3,2,1,0:T(8,128)} %bitcast.30, f32[2,4,8,64]{3,2,1,0:T(8,128)} %bitcast.31, bf16[512,2048]{1,0:T(8,128)(2,1)} %bitcast.25, ...), custom_call_target="tpu_custom_call" | custom-call | flops 49999998976 | bytes 200000000 | tf_op jit(solution)/shard_map/pallas_call | solution.py:592
  173.4 3.2 %copy.16 = bf16[1,2,4,64,2048]{4,3,2,1,0:T(8,128)(2,1)} copy(bf16[1,2,4,64,2048]{4,3,2,1,0:T(8,128)(2,1)} %bitcast.19) | data formatting | bytes 4194304

commit v5 on v4

--- a/solution.py
+++ b/solution.py
@@ -367,66 +367,85 @@
     span_q = 128
     score_scale = 1.0 / math.sqrt(head_dim)
 
-    spans = [(slice(r * span_q, (r + 1) * span_q), slice(h * head_dim, (h + 1) * head_dim))
-             for r in range(tok // span_q) for h in range(width // head_dim)]
-
-    def project(g, slot, kind):
-        qkv[slot, kind] = dot(xn[...], pool_in[g % ways, kind]).astype(BF16)
-
-    def score(slot):
+    def bounds(grps):
+        return grps[0] * group, len(grps) * group
+
+    def spans(count):
+        return [(slice(r * span_q, (r + 1) * span_q), slice(h * head_dim, (h + 1) * head_dim))
+                for r in range(count // span_q) for h in range(width // head_dim)]
+
+    def project(g, slot, kind, grps, shift):
+        lo, count = bounds(grps)
+        qkv[slot, kind, :count] = dot(xn[lo:lo + count], pool_in[(g + shift) % ways, kind]).astype(BF16)
+
+    def score(slot, count):
         row = lax.broadcasted_iota(jnp.int32, (span_q, span_q), 0)
         col = lax.broadcasted_iota(jnp.int32, (span_q, span_q), 1)
         visible = (row >= col) & (row // seq_len == col // seq_len)
         scores = []
-        for span in spans:
+        for span in spans(count):
             product = lax.dot_general(qkv[(slot, 0) + span], qkv[(slot, 1) + span], (((1,), (1,)), ((), ())), preferred_element_type=F32)
             scores.append(jnp.where(visible, product * score_scale, -1e30))
         return scores
 
-    def weigh(slot, scores):
+    def weigh(scores):
         weighed = []
         for values in scores:
             probs = jnp.exp(values - jnp.max(values, axis=-1, keepdims=True))
             weighed.append((probs.astype(BF16), jnp.sum(probs, axis=-1, keepdims=True)))
-        for span, (probs, total) in zip(spans, weighed):
+        return weighed
+
+    def gather_values(slot, weighed, count):
+        for span, (probs, total) in zip(spans(count), weighed):
             mixed[(slot,) + span] = (dot(probs, qkv[(slot, 2) + span]) / total).astype(BF16)
 
-    def project_out(g, slot):
+    def project_out(g, slot, grps, shift):
+        lo, count = bounds(grps)
         for n in range(dim // (2 * width)):
             span = pl.ds(n * 2 * width, 2 * width)
-            acc[:, span] += dot(mixed[slot], pool_out[g % ways, :, span])
-
-    def advance(g, slot):
-        for copy in in_loads(g, g % ways):
+            acc[lo:lo + count, span] += dot(mixed[slot, :count], pool_out[(g + shift) % ways, :, span])
+
+    def advance(g, slot, grps, shift, again):
+        lo, count = bounds(grps)
+        last = 1 - slot
+        for copy in in_loads(g, (g + shift) % ways):
             copy.wait()
-        out_load(g - 1, (g - 1) % ways).wait()
-        project(g, slot, 0)
-        scores = score(1 - slot)
-        project(g, slot, 1)
-        weigh(1 - slot, scores)
-        project(g, slot, 2)
-        project_out(g - 1, 1 - slot)
-
-        @pl.when(g + ways < head_groups)
+        out_load(g - 1, (g - 1 + shift) % ways).wait()
+        if count == span_q:
+            scores = score(last, count)
+            project(g, slot, 0, grps, shift)
+            weighed = weigh(scores)
+            project(g, slot, 1, grps, shift)
+            gather_values(last, weighed, count)
+        else:
+            project(g, slot, 0, grps, shift)
+            scores = score(last, count)
+            project(g, slot, 1, grps, shift)
+            gather_values(last, weigh(scores), count)
+        project(g, slot, 2, grps, shift)
+        project_out(g - 1, last, grps, shift)
+
+        @pl.when(again | (g + ways < head_groups))
         def _():
-            for copy in in_loads(g + ways, g % ways):
+            for copy in in_loads((g + ways) % head_groups, (g + shift) % ways):
                 copy.start()
 
-        @pl.when(g - 1 + ways < head_groups)
+        @pl.when(again | (g - 1 + ways < head_groups))
         def _():
-            out_load(g - 1 + ways, (g - 1) % ways).start()
-
-    def attend(g0, pairs):
+            out_load((g - 1 + ways) % head_groups, (g - 1 + shift) % ways).start()
+
+    def attend(g0, pairs, grps, shift, again):
         def body(i, _):
-            advance(g0 + 2 * i, g0 % 2)
-            advance(g0 + 2 * i + 1, 1 - g0 % 2)
+            advance(g0 + 2 * i, g0 % 2, grps, shift, again)
+            advance(g0 + 2 * i + 1, 1 - g0 % 2, grps, shift, again)
             return 0
 
         with jax.named_scope("attend"):
             lax.fori_loop(0, pairs, body, 0)
 
-    def out_copy(m):
-        return pltpu.make_async_copy(xn, out.at[m], out_sem.at[m])
+    def out_copy(m, grps):
+        part = pl.ds(*bounds(grps))
+        return pltpu.make_async_copy(xn.at[part], out.at[m, part], out_sem.at[m, grps[0]])
 
     def take_y(m, grp, q):
         y_copy(m, grp, q).wait_recv()
@@ -440,28 +459,32 @@
 
         lax.fori_loop(0, tok // 16, clear, 0)
 
-    def begin_attention():
-        for copy in in_loads(0, 0):
+    def begin_attention(grps, shift):
+        for copy in in_loads(0, shift % ways):
             copy.wait()
         for kind in range(3):
-            project(0, 0, kind)
-        for copy in in_loads(ways, 0):
+            project(0, 0, kind, grps, shift)
+        for copy in in_loads(ways, shift % ways):
             copy.start()
 
-    def end_attention(m):
-        advance(head_groups - 1, 1)
-        out_load(head_groups - 1, (head_groups - 1) % ways).wait()
-        weigh(1, score(1))
-        project_out(head_groups - 1, 1)
+    def end_attention(m, grps, shift, again):
+        lo, count = bounds(grps)
+        final = head_groups - 1
+        advance(final, 1, grps, shift, again)
+        out_load(final, (final + shift) % ways).wait()
+        gather_values(1, weigh(score(1, count)), count)
+        project_out(final, 1, grps, shift)
+        if again:
+            out_load((final + ways) % head_groups, (final + shift) % ways).start()
 
         def body(b, _):
-            r0 = pl.multiple_of(b * 16, 16)
+            r0 = pl.multiple_of(lo + b * 16, 16)
             proj = acc[pl.ds(r0, 16), :].astype(BF16).astype(F32)
             xn[pl.ds(r0, 16), :] = (y_in[m, pl.ds(r0, 16), :].astype(F32) + proj).astype(BF16)
             return 0
 
-        lax.fori_loop(0, tok // 16, body, 0)
-        out_copy(m).start()
+        lax.fori_loop(0, count // 16, body, 0)
+        out_copy(m, grps).start()
 
     def scoped(name, task, *args):
         with jax.named_scope(name):
@@ -522,28 +545,31 @@
     for grp in range(GROUPS):
         for q in range(seqs):
             scoped("take_y", take_y, 0, grp, q)
-    scoped("begin", begin_attention)
-    attend(1, 3)
+    scoped("begin", begin_attention, (0, 1), 0)
+    attend(1, 3, (0, 1), 0, True)
     scoped("arrive", arrive, 1, 1, 1, 1)
     whole(14, pbuf.at[1])
     whole(15, pbuf.at[1])
-    scoped("end", end_attention, 0)
-    prefetch()
+    scoped("end", end_attention, 0, (0, 1), 0, True)
     scoped("arrive", arrive, 1, 2, 0, 0)
     scoped("arrive", arrive, 1, 2, 1, 0)
-    out_copy(0).wait()
+    out_copy(0, (0, 1)).wait()
     clear_sums()
     scoped("final", arrive, 1, 3, 0, 1)
     scoped("take_y", take_y, 1, 0, 0)
     scoped("final", arrive, 1, 3, 1, 1, (0,))
     scoped("take_y", take_y, 1, 0, 1)
+    scoped("begin", begin_attention, (0,), head_groups)
     scoped("final", arrive, 1, 3, 1, 1, (1,))
+    attend(1, 3, (0,), head_groups, True)
+    scoped("end", end_attention, 1, (0,), head_groups, True)
     scoped("take_y", take_y, 1, 1, 0)
     scoped("take_y", take_y, 1, 1, 1)
-    scoped("begin", begin_attention)
-    attend(1, 3)
-    scoped("end", end_attention, 1)
-    scoped("out", out_copy(1).wait)
+    scoped("begin", begin_attention, (1,), 2 * head_groups)
+    attend(1, 3, (1,), 2 * head_groups, False)
+    scoped("end", end_attention, 1, (1,), 2 * head_groups, False)
+    for grp in range(GROUPS):
+        scoped("out", out_copy(1, (grp,)).wait)
 
     for m in range(micros):
         for s, b in peers:
@@ -624,7 +650,7 @@
                 dma((micros, chips - 1, GROUPS, CORES, seqs // GROUPS)), dma((micros, chips - 1, GROUPS, CORES, seqs // GROUPS)),
                 dma((micros, GROUPS, seqs // GROUPS)), dma((micros, GROUPS, seqs // GROUPS)),
                 dma((micros, GROUPS, seqs // GROUPS)), dma((micros, GROUPS, seqs // GROUPS)),
-                dma((micros, chips, CORES)), dma((micros, chips, CORES)), dma((3, 4)), dma((3,)), dma((3,)), dma((micros,)), dma((1,)),
+                dma((micros, chips, CORES)), dma((micros, chips, CORES)), dma((3, 4)), dma((3,)), dma((3,)), dma((micros, GROUPS)), dma((1,)),
                 pltpu.SemaphoreType.REGULAR((chips,)),
             ],
             compiler_params=pltpu.CompilerParams(collective_id=0, has_side_effects=True, vmem_limit_bytes=67_000_000),

time: 178 us -> 175 us (0.983)
  Pallas kernels: 173 us -> 171 us
    pallas_call x1, Pallas kernels: 173 us -> 171 us  [device_step(): pl.pallas_call(functools.partial(boundary_kernel, stages, ep_size, seq_le...]
where the time goes in v5:
time: 175 us
  Pallas kernels  171 us (98%)
  local copies, waits for them, and re-layouts  3.16 us (2%)
    pallas_call x1, Pallas kernels, device_step(): pl.pallas_call(functools.partial(boundary_kernel, stages, ep_size, seq_le...  171 us

profile of v5, /device:TPU:97, one launch (start us, length us, event | category | flops | bytes accessed | tf_op | source)
XLA Modules:
  0.0 174.6 jit_solution(16102848009203254518)
XLA Ops:
  0.0 171.4 %shard_map.136 = (bf16[2,256,2048]{2,1,0:T(8,128)(2,1)}, bf16[3,8,2048,256]{3,2,1,0:T(8,128)(2,1)}) custom-call(bf16[2,32,128,2048]{3,2,1,0:T(8,128)(2,1)} %bitcast.20, s32[2,4,8,64]{3,2,1,0:T(8,128)} %bitcast.29, s32[2,4,8,64]{3,2,1,0:T(8,128)} %bitcast.30, f32[2,4,8,64]{3,2,1,0:T(8,128)} %bitcast.31, bf16[512,2048]{1,0:T(8,128)(2,1)} %bitcast.25, ...), custom_call_target="tpu_custom_call" | custom-call | flops 49999998976 | bytes 200000000 | tf_op jit(solution)/shard_map/pallas_call | solution.py:618
  171.4 3.2 %copy.16 = bf16[1,2,4,64,2048]{4,3,2,1,0:T(8,128)(2,1)} copy(bf16[1,2,4,64,2048]{4,3,2,1,0:T(8,128)(2,1)} %bitcast.19) | data formatting | bytes 4194304
